TPU v7x, 32 devices: a whole 2x2x4 slice. The times are simulated.
32 devices in a mesh: gx: 8 (over z, y), gy: 4 (over x, core).
Axes of the slice: x: 2, y: 2, z: 4, core: 2. Of those that a mesh axis runs over, the one named last changes fastest.
Arguments:
- populations: float32 [27, 16, 32, 128], P(None, 'gx', 'gy'), as said below
- relax: float32 [27], replicated, may hold values from 0.6 to 1.9
- solid: int32 [16, 32, 128], P('gx', 'gy'), may hold values 0 or 1
- wall_cell: int32 [8, 4, 256], P('gx', 'gy'), may hold values from 0 to 2047, as said below
- wall_normal: int32 [8, 4, 256], P('gx', 'gy'), may hold values from 0 to 5
- wall_count: int32 [8, 4], P('gx', 'gy'), may hold values from 1 to 256, as said below
- sample_ref: int32 [8, 4, 256], P('gx', 'gy'), may hold values from 0 to 255, each once within a row
- stencil_cell: int32 [8, 4, 8, 256], P('gx', 'gy'), may hold values from 0 to 2047, as said below
- stencil_weight: float32 [8, 4, 8, 256], P('gx', 'gy'), may hold values from 0 to 1, as said below
Outputs:
- read: float32 [27, 16, 32, 128], P(None, 'gx', 'gy')
Inputs may be any that keep to these rules, and one draw needn't show every extreme that they name: `populations`: positive everywhere. `wall_cell`: the 256 entries of one device are distinct local cells. Slots 0 to wall_count - 1 of a device are live; some device has all 256 live. `stencil_cell`: the eight corners of a unit cube of the owner's local cells, wrapping along z only. `stencil_weight`: nonnegative trilinear weights, summing to one over the eight corners.
All inputs are finite; a program needn't handle non-finite values. No bound on the sum of `solid` on one device may be relied on, other than what follows from the above.
Results may differ from a plain program's by a relative error of at most 0.0003.
Values sent between devices are 32-bit elements; how exact they have to be, the bound alone decides.
No kernel may reach another device: no remote copies, remote signals or barrier semaphores. Data moves between devices by JAX's collectives and lax.ppermute only.
A program may use at most 64 MiB of HBM per device.

v0:
```python
import jax
import jax.numpy as jnp
import numpy as np
from jax import lax
from jax.sharding import PartitionSpec as P

lattice_steps = [(a - 1, b - 1, c - 1) for a in range(3) for b in range(3) for c in range(3)]
wall_ratio = (1.0 / 9.0) ** (1.0 / 7.0)


def padded_2(shard, sides, width):
    for axis, dim in sides:
        devices, length = (lax.axis_size(axis), shard.shape[dim])
        up = [(i, (i + 1) % devices) for i in range(devices)]
        down = [(j, i) for i, j in up]
        last = lax.slice_in_dim(shard, length - width, length, axis=dim)
        initial = lax.slice_in_dim(shard, 0, width, axis=dim)
        before = lax.ppermute(last, axis, up)
        after = lax.ppermute(initial, axis, down)
        shard = jnp.concatenate([before, shard, after], axis=dim)
    return shard


def lattice():
    steps = np.array(lattice_steps).T
    single = np.where(steps == 0, 2.0 / 3.0, 1.0 / 6.0)
    weights = np.prod(single, axis=0)
    vander = np.array([[1.0, 1.0, 1.0], [-1.0, 0.0, 1.0], [1.0, 0.0, 1.0]])
    undo = np.array([[0.0, -0.5, 0.5], [1.0, 0.0, -1.0], [0.0, 0.5, 0.5]])
    moment = np.kron(np.kron(vander, vander), vander)
    inverse = np.kron(np.kron(undo, undo), undo)
    return (
        jnp.asarray(steps, jnp.float32),
        jnp.asarray(weights, jnp.float32),
        jnp.asarray(moment, jnp.float32),
        jnp.asarray(inverse, jnp.float32),
    )


def moments(pops):
    steps, weights, moment, inverse = lattice()
    scaled = weights[:, None] * pops
    density = jnp.sum(scaled, axis=0)
    momentum = jnp.dot(steps, scaled, precision=lax.Precision.HIGHEST)
    return (density, momentum / density[None])


def equilibrium(density, velocity):
    steps, weights, moment, inverse = lattice()
    projected = jnp.dot(steps.T, velocity, precision=lax.Precision.HIGHEST)
    speed_sq = jnp.sum(velocity * velocity, axis=0)
    return density[None] * (
        1.0 + 3.0 * projected + 4.5 * projected * projected - 1.5 * speed_sq[None]
    )


def collide(pops, relax):
    steps, weights, moment, inverse = lattice()
    scaled = weights[:, None] * pops
    density, velocity = moments(pops)
    balance = weights[:, None] * equilibrium(density, velocity)
    deviation = jnp.dot(moment, scaled - balance, precision=lax.Precision.HIGHEST) * relax[:, None]
    after = scaled - jnp.dot(inverse, deviation, precision=lax.Precision.HIGHEST)
    return after / weights[:, None]


def sample_velocity(velocity, corner_cells, corner_weight):
    picked = velocity[:, corner_cells]
    return jnp.sum(picked * corner_weight[None], axis=1)


def rebuild_columns(columns, density, velocity, normal, live, picked):
    axis_index = normal // 2
    sign = (2 * (normal % 2) - 1).astype(jnp.float32)
    normal_vec = (jnp.arange(3, dtype=jnp.int32)[:, None] == axis_index[None]).astype(
        jnp.float32
    ) * sign[None]
    along = jnp.sum(picked * normal_vec, axis=0)
    tangential = picked - along[None] * normal_vec
    wall_eq = equilibrium(density, wall_ratio * tangential)
    local_eq = equilibrium(density, velocity)
    return jnp.where(live[None], wall_eq + columns - local_eq, columns)


def stream(padded, post):
    chans, size_x, size_y, size_z = post.shape
    outputs = []
    for direction in range(27):
        step_x, step_y, step_z = lattice_steps[direction]
        moved = padded[
            direction, 1 - step_x : 1 - step_x + size_x, 1 - step_y : 1 - step_y + size_y
        ]
        blocked = padded[27, 1 - step_x : 1 - step_x + size_x, 1 - step_y : 1 - step_y + size_y]
        moved = jnp.roll(moved, step_z, axis=2)
        blocked = jnp.roll(blocked, step_z, axis=2)
        outputs.append(jnp.where(blocked > 0.5, post[26 - direction], moved))
    return jnp.stack(outputs)


def local(
    populations,
    relax,
    solid,
    wall_cell,
    wall_normal,
    wall_count,
    sample_ref,
    stencil_cell,
    stencil_weight,
):
    chans, size_x, size_y, size_z = populations.shape
    flat = populations.reshape(27, size_x * size_y * size_z)
    density, velocity = moments(flat)
    samples = sample_velocity(velocity, stencil_cell[0, 0], stencil_weight[0, 0])
    peers = lax.axis_size("gy")
    received = lax.all_to_all(
        samples.reshape(3, peers, -1), "gy", split_axis=1, concat_axis=1, tiled=True
    ).reshape(3, -1)
    picked = received[:, sample_ref[0, 0]]
    walls = wall_cell[0, 0]
    normal = wall_normal[0, 0]
    live = jnp.arange(walls.shape[0], dtype=jnp.int32) < wall_count[0, 0]
    columns = rebuild_columns(
        flat[:, walls], density[walls], velocity[:, walls], normal, live, picked
    )
    post = collide(flat.at[:, walls].set(columns), relax)
    post_grid = post.reshape(27, size_x, size_y, size_z)
    stacked = jnp.concatenate([post_grid, solid.astype(jnp.float32)[None]], axis=0)
    padded = padded_2(stacked, (("gx", 1), ("gy", 2)), 1)
    return stream(padded, post_grid)


def solution(mesh):
    return jax.shard_map(
        local,
        mesh=mesh,
        in_specs=(
            P(None, "gx", "gy", None),
            P(),
            P("gx", "gy", None),
            P("gx", "gy", None),
            P("gx", "gy", None),
            P("gx", "gy"),
            P("gx", "gy", None),
            P("gx", "gy", None, None),
            P("gx", "gy", None, None),
        ),
        out_specs=P(None, "gx", "gy", None),
        check_vma=False,
    )
```

profile of v0, /device:TPU:1, one launch (start us, length us, event | category | flops | bytes accessed | tf_op | source)
XLA Modules:
  0.0 49.5 jit_solution(3774565193325353497)
XLA Ops:
  0.0 1.0 %pad.253 = f32[32,16,128]{2,1,0:T(8,128)S(1)} pad(f32[27,16,128]{2,1,0:T(8,128)} %bitcast.286, f32[]{:T(128)} %constant.24.clone.1), padding=0_5x0_0x0_0 | pad | bytes 483332
  1.1 0.8 %copy-done = f32[27,2,8,128]{3,2,1,0:T(8,128)S(1)} copy-done((f32[27,2,8,128]{3,2,1,0:T(8,128)S(1)}, f32[27,2,8,128]{3,2,1,0:T(8,128)}, u32[]{:S(2)}) %copy-start) | copy-done | bytes 221208
  2.0 0.7 %copy-done.1 = f32[3,27]{1,0:T(4,128)S(1)} copy-done((f32[3,27]{1,0:T(4,128)S(1)}, f32[3,27]{1,0:T(4,128)}, u32[]{:S(2)}) %copy-start.1) | copy-done | bytes 348
  3.0 0.4 copy.195
  3.8 5.5 %gather_fusion.1 = f32[2048,3]{1,0:T(8,128)S(1)} fusion(f32[3,2048]{0,1:T(8,128)S(1)} %copy.195, s32[2048]{0:T(1024)S(1)} %broadcast_clamp_fusion), kind=kCustom, calls=%fused_computation.1 | custom fusion | bytes 57344 | tf_op jit(solution)/shard_map/gather | solution.py:68
  9.7 0.7 %reshape.1466 = f32[4,1,192]{2,1,0:T(1,128)} reshape(f32[4,3,64]{2,1,0:T(4,128)S(1)} %bitcast.304) | data formatting | bytes 6144
  10.4 4.2 %all-to-all-start = ((f32[4,1,192]{2,1,0:T(1,128)}), f32[4,1,192]{2,1,0:T(1,128)S(1)}, u32[]{:S(2)}, u32[]{:S(2)}) async-start(f32[4,1,192]{2,1,0:T(1,128)} %reshape.1466), calls=%async_computation | async-start | bytes 8192 | tf_op jit(solution)/shard_map/all_to_all | solution.py:116
  14.8 0.6 %copy-done.8 = s32[1,1,256]{2,1,0:T(1,128)S(1)} copy-done((s32[1,1,256]{2,1,0:T(1,128)S(1)}, s32[1,1,256]{2,1,0:T(1,128)}, u32[]{:S(2)}) %copy-start.8) | copy-done | bytes 1048
  15.4 0.7 %copy-done.9 = s32[1,1,256]{2,1,0:T(1,128)S(1)} copy-done((s32[1,1,256]{2,1,0:T(1,128)S(1)}, s32[1,1,256]{2,1,0:T(1,128)}, u32[]{:S(2)}) %copy-start.9) | copy-done | bytes 1048
  16.1 0.7 %copy-done.7 = s32[1,1,256]{2,1,0:T(1,128)S(1)} copy-done((s32[1,1,256]{2,1,0:T(1,128)S(1)}, s32[1,1,256]{2,1,0:T(1,128)}, u32[]{:S(2)}) %copy-start.7) | copy-done | bytes 1048
  16.8 0.7 %gather_fusion.4 = f32[256,3]{1,0:T(8,128)S(1)} fusion(f32[3,2048]{0,1:T(8,128)S(1)} %copy.195, s32[1024]{0:T(1024)S(1)} %get-tuple-element.108), kind=kCustom, calls=%fused_computation.4 | custom fusion | bytes 7168 | tf_op jit(solution)/shard_map/gather | solution.py:124
  18.3 0.4 copy.202
  18.7 1.7 %gather_fusion = f32[256]{0:T(256)S(1)} fusion(f32[2048]{0:T(1024)S(1)} %bitcast.279, s32[1024]{0:T(1024)S(1)} %get-tuple-element.108), kind=kCustom, calls=%fused_computation | custom fusion | bytes 3072 | tf_op jit(solution)/shard_map/gather | solution.py:124
  20.4 0.7 %gather_fusion.3 = f32[256,27]{1,0:T(8,128)S(1)} fusion(f32[27,2048]{0,1:T(8,128)S(1)} %copy.202, s32[1024]{0:T(1024)S(1)} %get-tuple-element.108), kind=kCustom, calls=%fused_computation.3 | custom fusion | bytes 56320 | tf_op jit(solution)/shard_map/gather | solution.py:124
  21.2 0.5 %broadcast.392 = f32[]{:T(128)} broadcast(f32[]{:T(128)} %constant.441), dimensions={} | broadcast | bytes 8 | tf_op jit(solution)/shard_map/all_to_all | solution.py:116
  21.7 0.7 %reduce.5 = f32[4,192]{1,0:T(4,128)S(1)} reduce(f32[4,1,192]{2,1,0:T(1,128)S(1)} %all-to-all-done, f32[]{:T(128)} %broadcast.392), dimensions={1}, to_apply=%all_to_all.3.reduce_sub_computation | reduce | bytes 6148 | tf_op jit(solution)/shard_map/all_to_all | solution.py:116
  22.6 0.7 %gather_fusion.2 = f32[256,3]{1,0:T(8,128)S(1)} fusion(f32[3,256]{0,1:T(8,128)S(1)} %bitcast.288, s32[1024]{0:T(1024)S(1)} %get-tuple-element.107), kind=kCustom, calls=%fused_computation.2 | custom fusion | bytes 7168 | tf_op jit(solution)/shard_map/gather | solution.py:119
  23.8 0.4 fusion.25
  24.6 1.6 %scatter_fusion = f32[27,2048]{0,1:T(8,128)S(1)} fusion(f32[27,2048]{0,1:T(8,128)S(1)} %copy.202, s32[256]{0:T(256)S(1)} %bitcast.324, f32[256,27]{1,0:T(8,128)S(1)} %copy.203), kind=kCustom, calls=%fused_computation.5 | custom fusion | bytes 83968 | tf_op jit(solution)/shard_map/scatter | solution.py:126
  26.6 0.4 multiply_reduce_fusion.5
  27.0 0.4 fusion.64
  27.5 0.7 %copy-done.13 = f32[27,27]{1,0:T(8,128)S(1)} copy-done((f32[27,27]{1,0:T(8,128)S(1)}, f32[27,27]{1,0:T(8,128)}, u32[]{:S(2)}) %copy-start.13) | copy-done | bytes 2940
  28.2 0.5 convolution_multiply_fusion
  28.9 0.3 fusion
  29.6 1.7 %collective-permute-start = (f32[28,1,8,128]{3,2,1,0:T(8,128)S(1)}, f32[28,1,8,128]{3,2,1,0:T(8,128)S(1)}, u32[]{:S(2)}, u32[]{:S(2)}) collective-permute-start(f32[28,1,8,128]{3,2,1,0:T(8,128)S(1)} %get-tuple-element.63), channel_id=1, source_target_pairs={{0,4},{4,8},{8,12},{12,16},{16,20},{20,24},{24,28},{28,0},{1,5},{5... | collective-permute-start | bytes 344072 | tf_op jit(solution)/shard_map/ppermute | solution.py:18
  31.4 3.1 %collective-permute-start.1 = (f32[28,1,8,128]{3,2,1,0:T(8,128)S(1)}, f32[28,1,8,128]{3,2,1,0:T(8,128)S(1)}, u32[]{:S(2)}, u32[]{:S(2)}) collective-permute-start(f32[28,1,8,128]{3,2,1,0:T(8,128)S(1)} %get-tuple-element.64), channel_id=1, source_target_pairs={{4,0},{8,4},{12,8},{16,12},{20,16},{24,20},{28,24},{0,28},{5,1},{9... | collective-permute-start | bytes 344072 | tf_op jit(solution)/shard_map/ppermute | solution.py:19
  34.5 3.4 %collective-permute-done = f32[28,1,8,128]{3,2,1,0:T(8,128)S(1)} collective-permute-done((f32[28,1,8,128]{3,2,1,0:T(8,128)S(1)}, f32[28,1,8,128]{3,2,1,0:T(8,128)S(1)}, u32[]{:S(2)}, u32[]{:S(2)}) %collective-permute-start) | collective-permute-done | bytes 114720 | tf_op jit(solution)/shard_map/ppermute | solution.py:18
  37.9 2.8 %collective-permute-start.3 = (f32[28,4,1,128]{3,2,1,0:T(1,128)S(1)}, f32[28,4,1,128]{3,2,1,0:T(1,128)S(1)}, u32[]{:S(2)}, u32[]{:S(2)}) collective-permute-start(f32[28,4,1,128]{3,2,1,0:T(1,128)S(1)} %get-tuple-element.27), channel_id=1, source_target_pairs={{0,1},{1,2},{2,3},{3,0},{4,5},{5,6},{6,7},{7,4},{8,9},{9,10},{10,1... | collective-permute-start | bytes 172040 | tf_op jit(solution)/shard_map/ppermute | solution.py:18
  40.8 1.2 %collective-permute-done.3 = f32[28,4,1,128]{3,2,1,0:T(1,128)S(1)} collective-permute-done((f32[28,4,1,128]{3,2,1,0:T(1,128)S(1)}, f32[28,4,1,128]{3,2,1,0:T(1,128)S(1)}, u32[]{:S(2)}, u32[]{:S(2)}) %collective-permute-start.3) | collective-permute-done | bytes 57376 | tf_op jit(solution)/shard_map/ppermute | solution.py:18
  42.1 2.3 %collective-permute-done.2 = f32[28,4,1,128]{3,2,1,0:T(1,128)S(1)} collective-permute-done((f32[28,4,1,128]{3,2,1,0:T(1,128)S(1)}, f32[28,4,1,128]{3,2,1,0:T(1,128)S(1)}, u32[]{:S(2)}, u32[]{:S(2)}) %collective-permute-start.2) | collective-permute-done | bytes 57376 | tf_op jit(solution)/shard_map/ppermute | solution.py:19
  48.3 0.6 %copy-done.11 = f32[27,2,8,128]{3,2,1,0:T(8,128)} copy-done((f32[27,2,8,128]{3,2,1,0:T(8,128)}, f32[27,2,8,128]{3,2,1,0:T(8,128)S(1)}, u32[]{:S(2)}) %copy-start.11) | copy-done | bytes 221208
  48.9 0.7 %constant_dynamic-update-slice_fusion = f32[27,2,8,128]{3,2,1,0:T(8,128)} fusion(f32[27,2,8,128]{3,2,1,0:T(8,128)} %copy-done.11, f32[1,2,8,128]{3,2,1,0:T(8,128)S(1)} %bitcast.306, f32[1,2,8,127]{3,2,1,0:T(8,128)S(1)} %slice_bitcast_fusion.1, f32[1,2,8,1]{3,2,1,0:T(8,128)S(1)} %slice_bitcast_fusion.2, f32[1,2,8,127]{3,2,1,0:T(8,128)S(1)} %get-tuple-element.67, ...), kind=kLoop, calls=%fused_computation.57 | loop fusion | flops 8192 | bytes 32768 | tf_op jit(solution)/shard_map/stack | solution.py:97
  (142 shorter events, 7.7 us)
Async XLA Ops:
  1.0 0.9 %copy-start = (f32[27,2,8,128]{3,2,1,0:T(8,128)S(1)}, f32[27,2,8,128]{3,2,1,0:T(8,128)}, u32[]{:S(2)}) copy-start(f32[27,2,8,128]{3,2,1,0:T(8,128)} %param.19) | copy-start | bytes 663556
  1.0 0.9 %copy-start.4 = (f32[27]{0:T(128)S(1)}, f32[27]{0:T(128)}, u32[]{:S(2)}) copy-start(f32[27]{0:T(128)} %constant.64.clone) | copy-start | bytes 328
  2.0 0.7 %copy-start.1 = (f32[3,27]{1,0:T(4,128)S(1)}, f32[3,27]{1,0:T(4,128)}, u32[]{:S(2)}) copy-start(f32[3,27]{1,0:T(4,128)} %constant.63.clone) | copy-start | bytes 976
  3.0 0.7 %copy-start.6 = (s32[1,1,8,256]{3,2,1,0:T(8,128)S(1)}, s32[1,1,8,256]{3,2,1,0:T(8,128)}, u32[]{:S(2)}) copy-start(s32[1,1,8,256]{3,2,1,0:T(8,128)} %param.26) | copy-start | bytes 24580
  3.8 5.5 %copy-start.3 = (f32[1,1,8,256]{3,2,1,0:T(8,128)S(1)}, f32[1,1,8,256]{3,2,1,0:T(8,128)}, u32[]{:S(2)}) copy-start(f32[1,1,8,256]{3,2,1,0:T(8,128)} %param.27) | copy-start | bytes 24580
  9.7 4.9 %copy-start.5 = (s32[2,8,128]{2,1,0:T(8,128)S(1)}, s32[2,8,128]{2,1,0:T(8,128)}, u32[]{:S(2)}) copy-start(s32[2,8,128]{2,1,0:T(8,128)} %param.21) | copy-start | bytes 24580
  10.4 10.8 %all-to-all-start = ((f32[4,1,192]{2,1,0:T(1,128)}), f32[4,1,192]{2,1,0:T(1,128)S(1)}, u32[]{:S(2)}, u32[]{:S(2)}) async-start(f32[4,1,192]{2,1,0:T(1,128)} %reshape.1466), calls=%async_computation | async-start | bytes 8192 | tf_op jit(solution)/shard_map/all_to_all | solution.py:116
  14.7 0.7 %copy-start.8 = (s32[1,1,256]{2,1,0:T(1,128)S(1)}, s32[1,1,256]{2,1,0:T(1,128)}, u32[]{:S(2)}) copy-start(s32[1,1,256]{2,1,0:T(1,128)} %param.22) | copy-start | bytes 3076
  15.4 0.7 %copy-start.9 = (s32[1,1,256]{2,1,0:T(1,128)S(1)}, s32[1,1,256]{2,1,0:T(1,128)}, u32[]{:S(2)}) copy-start(s32[1,1,256]{2,1,0:T(1,128)} %param.25) | copy-start | bytes 3076
  16.1 0.7 %copy-start.7 = (s32[1,1,256]{2,1,0:T(1,128)S(1)}, s32[1,1,256]{2,1,0:T(1,128)}, u32[]{:S(2)}) copy-start(s32[1,1,256]{2,1,0:T(1,128)} %param.23) | copy-start | bytes 3076
  27.5 0.7 %copy-start.13 = (f32[27,27]{1,0:T(8,128)S(1)}, f32[27,27]{1,0:T(8,128)}, u32[]{:S(2)}) copy-start(f32[27,27]{1,0:T(8,128)} %constant.65.clone) | copy-start | bytes 8752
  27.5 0.7 %copy-start.12 = (f32[27]{0:T(128)S(1)}, f32[27]{0:T(128)}, u32[]{:S(2)}) copy-start(f32[27]{0:T(128)} %param.20) | copy-start | bytes 328
  28.2 0.7 %copy-start.2 = (f32[27,27]{1,0:T(8,128)S(1)}, f32[27,27]{1,0:T(8,128)}, u32[]{:S(2)}) copy-start(f32[27,27]{1,0:T(8,128)} %constant.66.clone) | copy-start | bytes 8752
  28.2 0.7 %copy-start.10 = (f32[27]{0:T(128)S(1)}, f32[27]{0:T(128)}, u32[]{:S(2)}) copy-start(f32[27]{0:T(128)} %constant.75) | copy-start | bytes 328
  29.6 8.2 %collective-permute-start = (f32[28,1,8,128]{3,2,1,0:T(8,128)S(1)}, f32[28,1,8,128]{3,2,1,0:T(8,128)S(1)}, u32[]{:S(2)}, u32[]{:S(2)}) collective-permute-start(f32[28,1,8,128]{3,2,1,0:T(8,128)S(1)} %get-tuple-element.63), channel_id=1, source_target_pairs={{0,4},{4,8},{8,12},{12,16},{16,20},{20,24},{24,28},{28,0},{1,5},{5... | collective-permute-start | bytes 344072 | tf_op jit(solution)/shard_map/ppermute | solution.py:18
  31.4 6.5 %collective-permute-start.1 = (f32[28,1,8,128]{3,2,1,0:T(8,128)S(1)}, f32[28,1,8,128]{3,2,1,0:T(8,128)S(1)}, u32[]{:S(2)}, u32[]{:S(2)}) collective-permute-start(f32[28,1,8,128]{3,2,1,0:T(8,128)S(1)} %get-tuple-element.64), channel_id=1, source_target_pairs={{4,0},{8,4},{12,8},{16,12},{20,16},{24,20},{28,24},{0,28},{5,1},{9... | collective-permute-start | bytes 344072 | tf_op jit(solution)/shard_map/ppermute | solution.py:19
  37.9 4.1 %collective-permute-start.3 = (f32[28,4,1,128]{3,2,1,0:T(1,128)S(1)}, f32[28,4,1,128]{3,2,1,0:T(1,128)S(1)}, u32[]{:S(2)}, u32[]{:S(2)}) collective-permute-start(f32[28,4,1,128]{3,2,1,0:T(1,128)S(1)} %get-tuple-element.27), channel_id=1, source_target_pairs={{0,1},{1,2},{2,3},{3,0},{4,5},{5,6},{6,7},{7,4},{8,9},{9,10},{10,1... | collective-permute-start | bytes 172040 | tf_op jit(solution)/shard_map/ppermute | solution.py:18
  40.8 3.6 %collective-permute-start.2 = (f32[28,4,1,128]{3,2,1,0:T(1,128)S(1)}, f32[28,4,1,128]{3,2,1,0:T(1,128)S(1)}, u32[]{:S(2)}, u32[]{:S(2)}) collective-permute-start(f32[28,4,1,128]{3,2,1,0:T(1,128)S(1)} %get-tuple-element.28), channel_id=1, source_target_pairs={{1,0},{2,1},{3,2},{0,3},{5,4},{6,5},{7,6},{4,7},{9,8},{10,9},{11,1... | collective-permute-start | bytes 172040 | tf_op jit(solution)/shard_map/ppermute | solution.py:19
  48.2 0.7 %copy-start.11 = (f32[27,2,8,128]{3,2,1,0:T(8,128)}, f32[27,2,8,128]{3,2,1,0:T(8,128)S(1)}, u32[]{:S(2)}) copy-start(f32[27,2,8,128]{3,2,1,0:T(8,128)S(1)} %get-tuple-element.6) | copy-start | bytes 663556
where the time goes:
time: 50 us; the launch traced here: 49.5 us
  local copies, waits for them, and re-layouts  22.9 us (46%)
  starting transfers between devices  11.9 us (24%)
  waiting for transfers between devices  6.92 us (14%)
  other arithmetic  4.04 us (8%)
  matrix products  2.63 us (5%)
  between operations  1.11 us (2%)
    unnamed x35, local copies, waits for them, and re-layouts  7.2 us
    gather x1, local copies, waits for them, and re-layouts, sample_velocity(): picked = velocity[:, corner_cells]  5.47 us
    ppermute x2, waiting for transfers between devices, padded_2(): before = lax.ppermute(last, axis, up)  4.58 us
    ppermute x2, starting transfers between devices, padded_2(): before = lax.ppermute(last, axis, up)  4.54 us
    all_to_all x1, starting transfers between devices, local(): lax.all_to_all(samples.reshape(3, peers, -1), 'gy', split_axis=1, concat_...  4.25 us
    ppermute x2, starting transfers between devices, padded_2(): after = lax.ppermute(initial, axis, down)  3.11 us
    ppermute x2, waiting for transfers between devices, padded_2(): after = lax.ppermute(initial, axis, down)  2.34 us
    scatter x2, local copies, waits for them, and re-layouts, local(): post = collide(flat.at[:, walls].set(columns), relax)  1.89 us
  transfers between devices with their start and end apart: 5, of which 3 were waited for; matrix products, arithmetic and copies ran while one was open for 8% of the time, Pallas kernels for 0%

commit v1 on v0

v1 whole, which is shorter than its diff:
```python
import jax
import jax.numpy as jnp
import numpy as np
from jax import lax
from jax.experimental import pallas as pl
from jax.experimental.pallas import tpu as pltpu
from jax.sharding import PartitionSpec as P

wall_ratio = (1.0 / 9.0) ** (1.0 / 7.0)
LANES = 128
ROWS = 8
RHO, VEL, REF, AXIS, SOLID, PLANES = 27, 28, 31, 32, 33, 34
FACE = 16
ANY = pl.BlockSpec(memory_space=pl.ANY)
VMEM = pl.BlockSpec(memory_space=pltpu.VMEM)


def direction(a, b, c):
    return 9 * a + 3 * b + c


def up(n):
    return -(-n // ROWS) * ROWS


def equilibria(density, velocity, wanted):
    ux, uy, uz = velocity
    rest = density * (1.0 - 1.5 * (ux * ux + uy * uy + uz * uz))
    out = {}
    for i in wanted:
        if i in out:
            continue
        step = (i // 9 - 1, i // 3 % 3 - 1, i % 3 - 1)
        along = None
        for s, u in zip(step, (ux, uy, uz)):
            if s:
                along = (u if s > 0 else -u) if along is None else (along + u if s > 0 else along - u)
        if along is None:
            out[i] = rest
            continue
        linear = density * along
        square = rest + 4.5 * (linear * along)
        out[i] = square + 3.0 * linear
        if 26 - i in wanted:
            out[26 - i] = square - 3.0 * linear
    return out


def along_axes(values, triple):
    for stride in (1, 3, 9):
        fresh = list(values)
        for i in range(27):
            if i // stride % 3 == 0:
                fresh[i], fresh[i + stride], fresh[i + 2 * stride] = triple(
                    values[i], values[i + stride], values[i + 2 * stride]
                )
        values = fresh
    return values


def relaxed(pops, relax):
    single = (1.0 / 6.0, 2.0 / 3.0, 1.0 / 6.0)
    weight = [single[i // 9] * single[i // 3 % 3] * single[i % 3] for i in range(27)]

    def raw(m, z, p):
        s = m + p
        return s + z, p - m, s

    def undo(m0, m1, m2):
        return m2 - m1, m0 - m2, m1 + m2

    moment = along_axes([w * p for w, p in zip(weight, pops)], raw)
    density = moment[0]
    inv = 1.0 / density
    vel = [moment[9] * inv, moment[3] * inv, moment[1] * inv]
    first = [moment[9], moment[3], moment[1]]
    second = [4.5 * (j * u) for j, u in zip(first, vel)]
    rest = density - (1.0 / 3.0) * (second[0] + second[1] + second[2])
    mu, nu, ka = (1.0, 0.0, 1.0 / 3.0), (0.0, 1.0 / 3.0, 0.0), (1.0 / 3.0, 0.0, 1.0 / 3.0)
    cross = {}
    kept = []
    for i in range(27):
        p = (i // 9, i // 3 % 3, i % 3)
        eq = None
        terms = [(mu[p[0]] * mu[p[1]] * mu[p[2]], rest)]
        for d in range(3):
            o, q = [e for e in range(3) if e != d]
            terms.append((3.0 * nu[p[d]] * mu[p[o]] * mu[p[q]], first[d]))
            terms.append((ka[p[d]] * mu[p[o]] * mu[p[q]], second[d]))
            factor = 9.0 * nu[p[o]] * nu[p[q]] * mu[p[d]]
            if factor:
                if d not in cross:
                    cross[d] = first[o] * vel[q]
                terms.append((factor, cross[d]))
        for f, t in terms:
            if f:
                t = t if abs(f - 1.0) < 1e-12 else f * t
                eq = t if eq is None else eq + t
        dev = moment[i] if eq is None else moment[i] - eq
        kept.append((1.0 - relax[i]) * dev)
    back = (3.0, 1.5, 3.0)
    kept = along_axes(kept, undo)
    kept = [back[i // 9] * back[i // 3 % 3] * back[i % 3] * k for i, k in enumerate(kept)]
    return density, vel, kept


def lanes_of(table, index):
    return jnp.take_along_axis(table, index, axis=1, mode="promise_in_bounds")


def first_kernel(
    pop_h, relax_h, solid_h, cell_h, normal_h, count_h, ref_h, scell_h, sweight_h,
    up_o, down_o, sample_o, state_o,
    pop, relax, solid, cell, normal, count, ref, scell, sweight, sems,
):
    size_x = pop.shape[1]
    walls, slots = cell.shape[1], scell.shape[1]
    moves = [
        (relax_h, relax), (count_h, count), (scell_h.at[0, 0], scell), (sweight_h.at[0, 0], sweight),
        (cell_h.at[0], cell), (normal_h.at[0], normal), (ref_h.at[0], ref), (pop_h, pop), (solid_h, solid),
    ]
    copies = [pltpu.make_async_copy(s, d, sems.at[n]) for n, (s, d) in enumerate(moves)]
    for copy in copies:
        copy.start()
    for copy in copies:
        copy.wait()
    rates = [relax[i] for i in range(27)]
    velocity = []
    for x in range(size_x):
        density, vel, kept = relaxed([pop[i, x] for i in range(27)], rates)
        velocity.append(vel)
        for i in range(27):
            state_o[i, x] = kept[i]
        state_o[RHO, x] = density
        for d in range(3):
            state_o[VEL + d, x] = vel[d]
        state_o[SOLID, x] = solid[x].astype(jnp.float32)
    sub = lax.broadcasted_iota(jnp.int32, (ROWS, LANES), 0)
    for t in range(slots // LANES):
        cells = scell[:, t * LANES : (t + 1) * LANES]
        weights = sweight[:, t * LANES : (t + 1) * LANES]
        row, z = cells // LANES, cells % LANES
        low = jnp.broadcast_to(z[0:1], (ROWS, LANES))
        other = z != low
        high = jnp.max(jnp.where(other, z, 0), axis=0, keepdims=True)
        high = jnp.broadcast_to(high, (ROWS, LANES))
        w_high = jnp.where(other, weights, 0.0)
        w_low = weights - w_high
        total = [jnp.zeros((ROWS, LANES), jnp.float32) for _ in range(3)]
        for x in range(size_x):
            a_low = jnp.zeros((ROWS, LANES), jnp.float32)
            a_high = a_low
            for k in range(8):
                hit = jnp.broadcast_to(row[k : k + 1], (ROWS, LANES)) == sub + x * ROWS
                a_low += jnp.where(hit, jnp.broadcast_to(w_low[k : k + 1], (ROWS, LANES)), 0.0)
                a_high += jnp.where(hit, jnp.broadcast_to(w_high[k : k + 1], (ROWS, LANES)), 0.0)
            for d in range(3):
                total[d] += a_low * lanes_of(velocity[x][d], low) + a_high * lanes_of(velocity[x][d], high)
        for d in range(3):
            r = d * (slots // LANES) + t
            line = jnp.sum(total[d], axis=0, keepdims=True)
            for o in (up_o, down_o, sample_o):
                o[r : r + 1, :] = line
    row, z = cell[...] // LANES, cell[...] % LANES
    live = lax.broadcasted_iota(jnp.int32, (1, walls), 1) < count[0, 0]
    low = jnp.where(live, ref[...] % LANES + 1, 0).astype(jnp.float32)
    high = jnp.where(live, ref[...] // LANES * 4 + normal[...] // 2, 0).astype(jnp.float32)
    height = size_x * ROWS
    at = lax.broadcasted_iota(jnp.int32, (height, walls), 0) == jnp.broadcast_to(row, (height, walls))
    left = jnp.concatenate(
        [jnp.where(at, jnp.broadcast_to(v, (height, walls)), 0.0) for v in (low, high)], axis=0
    ).astype(jnp.bfloat16)
    hot = lax.broadcasted_iota(jnp.int32, (LANES, walls), 0) == jnp.broadcast_to(z, (LANES, walls))
    hot = jnp.where(hot, 1.0, 0.0).astype(jnp.bfloat16)
    dense = lax.dot_general(left, hot, (((1,), (1,)), ((), ())), preferred_element_type=jnp.float32)
    for x in range(size_x):
        low = dense[x * ROWS : (x + 1) * ROWS].astype(jnp.int32)
        high = dense[height + x * ROWS : height + (x + 1) * ROWS].astype(jnp.int32)
        state_o[REF, x] = ((high // 4) * LANES + low - 1).astype(jnp.float32)
        state_o[AXIS, x] = (high % 4).astype(jnp.float32)
    base = up(3 * (slots // LANES))
    for o, b, y in ((up_o, 2, ROWS - 1), (down_o, 0, 0)):
        planes = [direction(a, b, c) for a in range(3) for c in range(3)] + list(range(RHO, PLANES))
        for n, plane in enumerate(planes):
            for x in range(size_x):
                r = base + n * size_x + x
                o[r : r + 1, :] = state_o[plane, x, y : y + 1, :]


def second_kernel(own, from_below, from_above, *rest, names, peers, slots, slots_each):
    state, rest = rest[0], rest[1:]
    far, outs = rest[: peers - 3], rest[peers - 3 :]
    post_o, edge_o, even_o, odd_o = outs
    gx, gy = names
    size_x = post_o.shape[1]
    width = slots // LANES
    base = up(3 * width)
    me = lax.axis_index(gy)
    parity = lax.axis_index(gx) % 2
    tables = [(own, me), (from_below, (me + peers - 1) % peers), (from_above, (me + 1) % peers)]
    for n, table in enumerate(far):
        tables.append((table, (me + peers - (n + 2)) % peers))

    def walled(block, ref, axis, vel):
        index = jnp.maximum(ref, 0)
        source = index // slots_each
        start = block * slots_each
        tile = start // LANES
        lane = start % LANES + index % slots_each
        out = []
        for d in range(3):
            picked = jnp.zeros(ref.shape, jnp.float32)
            for table, who in tables:
                line = table[pl.ds(d * width + tile, 1), :]
                got = lanes_of(jnp.broadcast_to(line, (ROWS, LANES)), lane)
                picked = jnp.where(source == who, got, picked)
            tangential = jnp.where(axis == d, 0.0, wall_ratio * picked)
            out.append(jnp.where(ref >= 0, tangential, vel[d]))
        return out

    plus, minus, corner_plus, corner_minus = [], [], [], []
    for x in range(size_x):
        ref = state[REF, x].astype(jnp.int32)
        axis = state[AXIS, x].astype(jnp.int32)
        vel = walled(me, ref, axis, [state[VEL + d, x] for d in range(3)])
        eq = equilibria(state[RHO, x], vel, range(27))
        for i in range(27):
            value = state[i, x] + eq[i]
            post_o[i, x] = value
            if x == size_x - 1 and i >= 18:
                plus.append(value)
            if x == 0 and i < 9:
                minus.append(value)
    plus.append(state[SOLID, size_x - 1])
    minus.append(state[SOLID, 0])
    sub = lax.broadcasted_iota(jnp.int32, (ROWS, LANES), 0)
    for side, (table, b, block) in enumerate(
        ((from_below, 2, (me + peers - 1) % peers), (from_above, 0, (me + 1) % peers))
    ):
        def plane(n):
            rows = [table[base + n * size_x + x : base + n * size_x + x + 1, :] for x in range(size_x)]
            tile = jnp.broadcast_to(rows[0], (ROWS, LANES))
            for x in range(1, size_x):
                tile = jnp.where(sub == x, jnp.broadcast_to(rows[x], (ROWS, LANES)), tile)
            return tile

        ref = plane(13).astype(jnp.int32)
        axis = plane(14).astype(jnp.int32)
        vel = walled(block, ref, axis, [plane(10 + d) for d in range(3)])
        wanted = [direction(a, b, c) for a in range(3) for c in range(3)]
        eq = equilibria(plane(9), vel, wanted)
        for n, i in enumerate(wanted):
            value = plane(n) + eq[i]
            r = (side * 10 + n) * size_x
            edge_o[r : r + size_x, :] = value[:size_x]
            if i >= 18:
                corner_plus.append(value[size_x - 1 : size_x])
            if i < 9:
                corner_minus.append(value[0:1])
        solid = plane(15)
        r = (side * 10 + 9) * size_x
        edge_o[r : r + size_x, :] = solid[:size_x]
        corner_plus.append(solid[size_x - 1 : size_x])
        corner_minus.append(solid[0:1])
    for n in range(10):
        even_o[n] = jnp.where(parity == 0, plus[n], minus[n])
        odd_o[n] = jnp.where(parity == 0, minus[n], plus[n])
    for n in range(8):
        even_o[10, n : n + 1, :] = jnp.where(parity == 0, corner_plus[n], corner_minus[n])
        odd_o[10, n : n + 1, :] = jnp.where(parity == 0, corner_minus[n], corner_plus[n])


def third_kernel(post, edge, state, even, odd, out_h, out, sems, *, names):
    gx, gy = names
    size_x = post.shape[1]
    parity = lax.axis_index(gx) % 2
    sub = lax.broadcasted_iota(jnp.int32, (ROWS, LANES), 0)

    def below(n):
        return jnp.where(parity == 0, odd[n], even[n])

    def above(n):
        return jnp.where(parity == 0, even[n], odd[n])

    corners = {-1: below(10), size_x: above(10)}

    def shifted(tile, row, step_y):
        if step_y == 0:
            return tile
        rolled = pltpu.roll(tile, step_y % ROWS, 0)
        return jnp.where(sub == (0 if step_y > 0 else ROWS - 1), jnp.broadcast_to(row, (ROWS, LANES)), rolled)

    def source(x, step_y, n_face, n_edge, n_corner, inside):
        side = 0 if step_y > 0 else 1
        if 0 <= x < size_x:
            tile = inside(x)
            r = (side * 10 + n_edge) * size_x + x
            row = edge[r : r + 1, :] if step_y else None
        else:
            tile = below(n_face) if x < 0 else above(n_face)
            row = corners[x][side * 4 + n_corner : side * 4 + n_corner + 1] if step_y else None
        return shifted(tile, row, step_y)

    copies = []
    for a in range(3):
        for b in range(3):
            for x in range(size_x):
                from_x, step_y = x - (a - 1), b - 1
                wall = source(from_x, step_y, 9, 9, 3, lambda q: state[SOLID, q])
                for c in range(3):
                    i = direction(a, b, c)
                    moved = source(from_x, step_y, 3 * b + c, 3 * a + c, c, lambda q: post[i, q])
                    solid = wall
                    if c != 1:
                        moved = pltpu.roll(moved, (c - 1) % LANES, 1)
                        solid = pltpu.roll(wall, (c - 1) % LANES, 1)
                    out[i, x] = jnp.where(solid > 0.5, post[26 - i, x], moved)
        copy = pltpu.make_async_copy(out.at[pl.ds(9 * a, 9)], out_h.at[pl.ds(9 * a, 9)], sems.at[a])
        copy.start()
        copies.append(copy)
    for copy in copies:
        copy.wait()


def local(
    populations, relax, solid, wall_cell, wall_normal, wall_count, sample_ref, stencil_cell, stencil_weight
):
    chans, size_x, size_y, size_z = populations.shape
    walls, slots = wall_cell.shape[-1], stencil_cell.shape[-1]
    devices, peers = lax.axis_size("gx"), lax.axis_size("gy")
    slots_each = slots // peers
    if (size_y, size_z) != (ROWS, LANES) or walls % LANES or slots % LANES:
        raise ValueError("unsupported block")
    if LANES % slots_each or devices % 2 or peers < 4:
        raise ValueError("unsupported mesh")
    f32 = jnp.float32
    lines = up(3 * (slots // LANES))
    face = (lines + FACE * size_x, LANES)
    block = (size_x, ROWS, LANES)
    up_face, down_face, samples, state = pl.pallas_call(
        first_kernel,
        out_shape=[
            jax.ShapeDtypeStruct(face, f32),
            jax.ShapeDtypeStruct(face, f32),
            jax.ShapeDtypeStruct((lines, LANES), f32),
            jax.ShapeDtypeStruct((PLANES, *block), f32),
        ],
        in_specs=[ANY] * 9,
        out_specs=[VMEM] * 4,
        scratch_shapes=[
            pltpu.VMEM(populations.shape, f32),
            pltpu.SMEM(relax.shape, f32),
            pltpu.VMEM(block, jnp.int32),
            pltpu.VMEM((1, walls), jnp.int32),
            pltpu.VMEM((1, walls), jnp.int32),
            pltpu.SMEM((1, 1), jnp.int32),
            pltpu.VMEM((1, walls), jnp.int32),
            pltpu.VMEM((8, slots), jnp.int32),
            pltpu.VMEM((8, slots), f32),
            pltpu.SemaphoreType.DMA((9,)),
        ],
        name="first",
    )(populations, relax, solid, wall_cell, wall_normal, wall_count, sample_ref, stencil_cell, stencil_weight)

    def shift(value, by):
        return lax.ppermute(value, "gy", [(i, (i + by) % peers) for i in range(peers)])

    from_below = shift(up_face, 1)
    from_above = shift(down_face, peers - 1)
    far = [shift(samples, n) for n in range(2, peers - 1)]
    names = ("gx", "gy")
    post, edge, even, odd = pl.pallas_call(
        lambda *refs: second_kernel(*refs, names=names, peers=peers, slots=slots, slots_each=slots_each),
        out_shape=[
            jax.ShapeDtypeStruct(populations.shape, f32),
            jax.ShapeDtypeStruct((up(20 * size_x), LANES), f32),
            jax.ShapeDtypeStruct((11, ROWS, LANES), f32),
            jax.ShapeDtypeStruct((11, ROWS, LANES), f32),
        ],
        in_specs=[VMEM] * (4 + len(far)),
        out_specs=[VMEM] * 4,
        name="second",
    )(samples, from_below, from_above, state, *far)
    swap_even = [(i, i ^ 1) for i in range(devices)]
    swap_odd = [(i, ((i - 1) ^ 1) + 1) for i in range(devices)]
    swap_odd = [(i, j % devices) for i, j in swap_odd]
    got_odd = lax.ppermute(odd, "gx", swap_odd)
    got_even = lax.ppermute(even, "gx", swap_even)
    return pl.pallas_call(
        lambda *refs: third_kernel(*refs, names=names),
        out_shape=jax.ShapeDtypeStruct(populations.shape, f32),
        in_specs=[VMEM] * 5,
        out_specs=ANY,
        scratch_shapes=[pltpu.VMEM(populations.shape, f32), pltpu.SemaphoreType.DMA((3,))],
        name="third",
    )(post, edge, state, got_even, got_odd)


def solution(mesh):
    return jax.shard_map(
        local,
        mesh=mesh,
        in_specs=(
            P(None, "gx", "gy", None),
            P(),
            P("gx", "gy", None),
            P("gx", "gy", None),
            P("gx", "gy", None),
            P("gx", "gy"),
            P("gx", "gy", None),
            P("gx", "gy", None, None),
            P("gx", "gy", None, None),
        ),
        out_specs=P(None, "gx", "gy", None),
        check_vma=False,
    )
```

time: 50 us -> 23.3 us (0.47)
  the two profiles are of different devices: /device:TPU:1 before, /device:TPU:0 now
where the time goes in v1:
time: 23.3 us; the launch traced here: 23.1 us
  starting transfers between devices  9.94 us (43%)
  Pallas kernels  5.84 us (25%)
  waiting for transfers between devices  5.42 us (23%)
  local copies, waits for them, and re-layouts  1.22 us (5%)
  between operations  0.69 us (3%)
    ppermute x3, starting transfers between devices, shift(): lax.ppermute(value, 'gy', [(i, (i + by) % peers) for i in range(peers)])  4.76 us
    ppermute x1, starting transfers between devices, local(): got_odd = lax.ppermute(odd, 'gx', swap_odd)  3.55 us
    ppermute x1, waiting for transfers between devices, local(): got_odd = lax.ppermute(odd, 'gx', swap_odd)  3.4 us
    pallas_call x1, Pallas kernels, local(): pl.pallas_call(first_kernel, out_shape=[jax.ShapeDtypeStruct(face, f32),...  2.1 us
    ppermute x3, waiting for transfers between devices, shift(): lax.ppermute(value, 'gy', [(i, (i + by) % peers) for i in range(peers)])  2.01 us
    pallas_call x1, Pallas kernels, local(): pl.pallas_call(lambda *refs: third_kernel(*refs, names=names), out_shape=...  1.91 us
    pallas_call x1, Pallas kernels, local(): pl.pallas_call(lambda *refs: second_kernel(*refs, names=names, peers=peer...  1.83 us
    ppermute x1, starting transfers between devices, local(): got_even = lax.ppermute(even, 'gx', swap_even)  1.63 us
  transfers between devices with their start and end apart: 5, of which 2 were waited for; matrix products, arithmetic and copies ran while one was open for 0% of the time, Pallas kernels for 0%

profile of v1, /device:TPU:0, one launch (start us, length us, event | category | flops | bytes accessed | tf_op | source)
XLA Modules:
  0.0 23.1 jit_solution(6506744799925460528)
XLA Ops:
  0.7 2.1 %first.1 = (f32[40,128]{1,0:T(8,128)}, f32[40,128]{1,0:T(8,128)}, f32[8,128]{1,0:T(8,128)}, f32[34,2,8,128]{3,2,1,0:T(8,128)}) custom-call(f32[27,2,8,128]{3,2,1,0:T(8,128)} %pop_h.1, f32[27]{0:T(128)} %relax_h.1, s32[2,8,128]{2,1,0:T(8,128)} %solid_h.1, s32[1,1,256]{2,1,0:T(1,128)} %cell_h.1, s32[1,1,256]{2,1,0:T(1,128)} %normal_h.1, ...), custom_call_target="tpu_custom_call" | custom-call | tf_op jit(solution)/shard_map/first/pallas_call | solution.py:340
  2.8 0.0 copy-start.4
  2.8 0.5 %collective-permute-start = (f32[40,128]{1,0:T(8,128)}, f32[40,128]{1,0:T(8,128)S(1)}, u32[]{:S(2)}, u32[]{:S(2)}) collective-permute-start(f32[40,128]{1,0:T(8,128)} %get-tuple-element.14), channel_id=1, source_target_pairs={{0,1},{1,2},{2,3},{3,0},{4,5},{5,6},{6,7},{7,4},{8,9},{9,10},{10,1... | collective-permute-start | bytes 61448 | tf_op jit(solution)/shard_map/ppermute | solution.py:366
  3.3 2.0 %collective-permute-start.1 = (f32[40,128]{1,0:T(8,128)}, f32[40,128]{1,0:T(8,128)S(1)}, u32[]{:S(2)}, u32[]{:S(2)}) collective-permute-start(f32[40,128]{1,0:T(8,128)} %get-tuple-element.15), channel_id=1, source_target_pairs={{0,3},{1,0},{2,1},{3,2},{4,7},{5,4},{6,5},{7,6},{8,11},{9,8},{10,9... | collective-permute-start | bytes 61448 | tf_op jit(solution)/shard_map/ppermute | solution.py:366
  5.3 0.0 copy-done.4
  5.3 2.2 %collective-permute-start.2 = (f32[8,128]{1,0:T(8,128)S(1)}, f32[8,128]{1,0:T(8,128)S(1)}, u32[]{:S(2)}, u32[]{:S(2)}) collective-permute-start(f32[8,128]{1,0:T(8,128)S(1)} %copy-done.4), channel_id=1, source_target_pairs={{0,2},{1,3},{2,0},{3,1},{4,6},{5,7},{6,4},{7,5},{8,10},{9,11},{10,... | collective-permute-start | bytes 12296 | tf_op jit(solution)/shard_map/ppermute | solution.py:366
  7.5 2.0 %collective-permute-done.2.refs_4_ = f32[8,128]{1,0:T(8,128)S(1)} collective-permute-done((f32[8,128]{1,0:T(8,128)S(1)}, f32[8,128]{1,0:T(8,128)S(1)}, u32[]{:S(2)}, u32[]{:S(2)}) %collective-permute-start.2) | collective-permute-done | bytes 4128 | tf_op jit(solution)/shard_map/ppermute | solution.py:366
  9.5 0.0 copy-start.5
  9.5 0.0 collective-permute-done.refs_1_
  9.6 0.0 copy-start.2
  9.6 0.0 collective-permute-done.1.refs_2_
  9.6 0.0 copy-start.3
  9.6 0.6 %copy-done.5 = f32[8,128]{1,0:T(8,128)} copy-done((f32[8,128]{1,0:T(8,128)}, f32[8,128]{1,0:T(8,128)S(1)}, u32[]{:S(2)}) %copy-start.5) | copy-done | bytes 4120
  10.1 0.0 copy-done.2
  10.1 0.0 copy-done.3
  10.2 1.8 %second.1 = (f32[27,2,8,128]{3,2,1,0:T(8,128)}, f32[40,128]{1,0:T(8,128)}, f32[11,8,128]{2,1,0:T(8,128)}, f32[11,8,128]{2,1,0:T(8,128)}) custom-call(f32[8,128]{1,0:T(8,128)} %get-tuple-element.13.refs_0_, f32[40,128]{1,0:T(8,128)} %copy-done.2, f32[40,128]{1,0:T(8,128)} %copy-done.3, f32[34,2,8,128]{3,2,1,0:T(8,128)} %get-tuple-element.16.refs_3_.refs_2_, ...), custom_call_target="tpu_custom_call" | custom-call | tf_op jit(solution)/shard_map/second/pallas_call | solution.py:372
  12.0 1.6 %collective-permute-start.3 = (f32[11,8,128]{2,1,0:T(8,128)}, f32[11,8,128]{2,1,0:T(8,128)S(1)}, u32[]{:S(2)}, u32[]{:S(2)}) collective-permute-start(f32[11,8,128]{2,1,0:T(8,128)} %get-tuple-element.19), channel_id=1, source_target_pairs={{0,4},{4,0},{8,12},{12,8},{16,20},{20,16},{24,28},{28,24},{1,5},{5... | collective-permute-start | bytes 135176 | tf_op jit(solution)/shard_map/ppermute | solution.py:388
  13.6 3.5 %collective-permute-start.4 = (f32[11,8,128]{2,1,0:T(8,128)}, f32[11,8,128]{2,1,0:T(8,128)S(1)}, u32[]{:S(2)}, u32[]{:S(2)}) collective-permute-start(f32[11,8,128]{2,1,0:T(8,128)} %get-tuple-element.20), channel_id=1, source_target_pairs={{0,28},{4,8},{8,4},{12,16},{16,12},{20,24},{24,20},{28,0},{1,29},{... | collective-permute-start | bytes 135176 | tf_op jit(solution)/shard_map/ppermute | solution.py:387
  17.2 0.0 collective-permute-done.3.refs_3_
  17.2 0.0 copy-start
  17.2 3.4 %collective-permute-done.4.refs_4_ = f32[11,8,128]{2,1,0:T(8,128)S(1)} collective-permute-done((f32[11,8,128]{2,1,0:T(8,128)}, f32[11,8,128]{2,1,0:T(8,128)S(1)}, u32[]{:S(2)}, u32[]{:S(2)}) %collective-permute-start.4) | collective-permute-done | bytes 45088 | tf_op jit(solution)/shard_map/ppermute | solution.py:387
  20.6 0.0 copy-start.1
  20.6 0.0 copy-done
  20.6 0.6 %copy-done.1 = f32[11,8,128]{2,1,0:T(8,128)} copy-done((f32[11,8,128]{2,1,0:T(8,128)}, f32[11,8,128]{2,1,0:T(8,128)S(1)}, u32[]{:S(2)}) %copy-start.1) | copy-done | bytes 45080
  21.2 1.9 %third.1 = f32[27,2,8,128]{3,2,1,0:T(8,128)} custom-call(f32[27,2,8,128]{3,2,1,0:T(8,128)} %get-tuple-element.17.refs_0_, f32[40,128]{1,0:T(8,128)} %get-tuple-element.18.refs_1_, f32[34,2,8,128]{3,2,1,0:T(8,128)} %get-tuple-element.16.refs_3_.refs_2_, f32[11,8,128]{2,1,0:T(8,128)} %copy-done, f32[11,8,128]{2,1,0:T(8,128)} %copy-done.1), custom_call_target="tpu_custom_call" | custom-call | tf_op jit(solution)/shard_map/third/pallas_call | solution.py:389
Async XLA Ops:
  2.8 2.5 %copy-start.4 = (f32[8,128]{1,0:T(8,128)S(1)}, f32[8,128]{1,0:T(8,128)}, u32[]{:S(2)}) copy-start(f32[8,128]{1,0:T(8,128)} %get-tuple-element.13.refs_0_) | copy-start | bytes 12292
  2.8 6.8 %collective-permute-start = (f32[40,128]{1,0:T(8,128)}, f32[40,128]{1,0:T(8,128)S(1)}, u32[]{:S(2)}, u32[]{:S(2)}) collective-permute-start(f32[40,128]{1,0:T(8,128)} %get-tuple-element.14), channel_id=1, source_target_pairs={{0,1},{1,2},{2,3},{3,0},{4,5},{5,6},{6,7},{7,4},{8,9},{9,10},{10,1... | collective-permute-start | bytes 61448 | tf_op jit(solution)/shard_map/ppermute | solution.py:366
  3.3 6.2 %collective-permute-start.1 = (f32[40,128]{1,0:T(8,128)}, f32[40,128]{1,0:T(8,128)S(1)}, u32[]{:S(2)}, u32[]{:S(2)}) collective-permute-start(f32[40,128]{1,0:T(8,128)} %get-tuple-element.15), channel_id=1, source_target_pairs={{0,3},{1,0},{2,1},{3,2},{4,7},{5,4},{6,5},{7,6},{8,11},{9,8},{10,9... | collective-permute-start | bytes 61448 | tf_op jit(solution)/shard_map/ppermute | solution.py:366
  5.3 4.3 %collective-permute-start.2 = (f32[8,128]{1,0:T(8,128)S(1)}, f32[8,128]{1,0:T(8,128)S(1)}, u32[]{:S(2)}, u32[]{:S(2)}) collective-permute-start(f32[8,128]{1,0:T(8,128)S(1)} %copy-done.4), channel_id=1, source_target_pairs={{0,2},{1,3},{2,0},{3,1},{4,6},{5,7},{6,4},{7,5},{8,10},{9,11},{10,... | collective-permute-start | bytes 12296 | tf_op jit(solution)/shard_map/ppermute | solution.py:366
  9.5 0.6 %copy-start.5 = (f32[8,128]{1,0:T(8,128)}, f32[8,128]{1,0:T(8,128)S(1)}, u32[]{:S(2)}) copy-start(f32[8,128]{1,0:T(8,128)S(1)} %collective-permute-done.2.refs_4_) | copy-start | bytes 12292
  9.6 0.6 %copy-start.2 = (f32[40,128]{1,0:T(8,128)}, f32[40,128]{1,0:T(8,128)S(1)}, u32[]{:S(2)}) copy-start(f32[40,128]{1,0:T(8,128)S(1)} %collective-permute-done.refs_1_) | copy-start | bytes 61444
  9.6 0.6 %copy-start.3 = (f32[40,128]{1,0:T(8,128)}, f32[40,128]{1,0:T(8,128)S(1)}, u32[]{:S(2)}) copy-start(f32[40,128]{1,0:T(8,128)S(1)} %collective-permute-done.1.refs_2_) | copy-start | bytes 61444
  12.0 5.2 %collective-permute-start.3 = (f32[11,8,128]{2,1,0:T(8,128)}, f32[11,8,128]{2,1,0:T(8,128)S(1)}, u32[]{:S(2)}, u32[]{:S(2)}) collective-permute-start(f32[11,8,128]{2,1,0:T(8,128)} %get-tuple-element.19), channel_id=1, source_target_pairs={{0,4},{4,0},{8,12},{12,8},{16,20},{20,16},{24,28},{28,24},{1,5},{5... | collective-permute-start | bytes 135176 | tf_op jit(solution)/shard_map/ppermute | solution.py:388
  13.6 7.0 %collective-permute-start.4 = (f32[11,8,128]{2,1,0:T(8,128)}, f32[11,8,128]{2,1,0:T(8,128)S(1)}, u32[]{:S(2)}, u32[]{:S(2)}) collective-permute-start(f32[11,8,128]{2,1,0:T(8,128)} %get-tuple-element.20), channel_id=1, source_target_pairs={{0,28},{4,8},{8,4},{12,16},{16,12},{20,24},{24,20},{28,0},{1,29},{... | collective-permute-start | bytes 135176 | tf_op jit(solution)/shard_map/ppermute | solution.py:387
  17.2 3.4 %copy-start = (f32[11,8,128]{2,1,0:T(8,128)}, f32[11,8,128]{2,1,0:T(8,128)S(1)}, u32[]{:S(2)}) copy-start(f32[11,8,128]{2,1,0:T(8,128)S(1)} %collective-permute-done.3.refs_3_) | copy-start | bytes 135172
  20.6 0.6 %copy-start.1 = (f32[11,8,128]{2,1,0:T(8,128)}, f32[11,8,128]{2,1,0:T(8,128)S(1)}, u32[]{:S(2)}) copy-start(f32[11,8,128]{2,1,0:T(8,128)S(1)} %collective-permute-done.4.refs_4_) | copy-start | bytes 135172

commit v2 on v1

--- a/solution.py
+++ b/solution.py
@@ -11,8 +11,9 @@
 ROWS = 8
 RHO, VEL, REF, AXIS, SOLID, PLANES = 27, 28, 31, 32, 33, 34
 FACE = 16
-ANY = pl.BlockSpec(memory_space=pl.ANY)
+HBM = pl.BlockSpec(memory_space=pltpu.HBM)
 VMEM = pl.BlockSpec(memory_space=pltpu.VMEM)
+GRANT = 4 * 1024 * 1024
 
 
 def direction(a, b, c):
@@ -345,7 +346,7 @@
             jax.ShapeDtypeStruct((lines, LANES), f32),
             jax.ShapeDtypeStruct((PLANES, *block), f32),
         ],
-        in_specs=[ANY] * 9,
+        in_specs=[HBM] * 9,
         out_specs=[VMEM] * 4,
         scratch_shapes=[
             pltpu.VMEM(populations.shape, f32),
@@ -359,8 +360,16 @@
             pltpu.VMEM((8, slots), f32),
             pltpu.SemaphoreType.DMA((9,)),
         ],
+        compiler_params=pltpu.CompilerParams(vmem_limit_bytes=GRANT),
         name="first",
-    )(populations, relax, solid, wall_cell, wall_normal, wall_count, sample_ref, stencil_cell, stencil_weight)
+    )(
+        *(
+            v if v is wall_count else pltpu.with_memory_space_constraint(v, pltpu.HBM)
+            for v in (
+                populations, relax, solid, wall_cell, wall_normal, wall_count, sample_ref, stencil_cell, stencil_weight
+            )
+        )
+    )
 
     def shift(value, by):
         return lax.ppermute(value, "gy", [(i, (i + by) % peers) for i in range(peers)])
@@ -379,6 +388,7 @@
         ],
         in_specs=[VMEM] * (4 + len(far)),
         out_specs=[VMEM] * 4,
+        compiler_params=pltpu.CompilerParams(vmem_limit_bytes=GRANT),
         name="second",
     )(samples, from_below, from_above, state, *far)
     swap_even = [(i, i ^ 1) for i in range(devices)]
@@ -390,8 +400,9 @@
         lambda *refs: third_kernel(*refs, names=names),
         out_shape=jax.ShapeDtypeStruct(populations.shape, f32),
         in_specs=[VMEM] * 5,
-        out_specs=ANY,
+        out_specs=HBM,
         scratch_shapes=[pltpu.VMEM(populations.shape, f32), pltpu.SemaphoreType.DMA((3,))],
+        compiler_params=pltpu.CompilerParams(vmem_limit_bytes=GRANT),
         name="third",
     )(post, edge, state, got_even, got_odd)
 

time: 23.3 us -> 18.4 us (0.79)
  Pallas kernels: 5.84 us -> 2.38 us
  local copies, waits for them, and re-layouts: 1.22 us -> 0 us
  waiting for transfers between devices: 5.42 us -> 5 us
  starting transfers between devices: 9.94 us -> 10.2 us
    pallas_call x1, Pallas kernels: 1.83 us -> 0.19 us  [local(): pl.pallas_call(lambda *refs: second_kernel(*refs, names=names, peers=peer...]
    unnamed x12 -> x0, local copies, waits for them, and re-layouts: 1.22 us -> none
    pallas_call x1, Pallas kernels: 1.91 us -> 0.81 us  [local(): pl.pallas_call(lambda *refs: third_kernel(*refs, names=names), out_shape=...]
    pallas_call x1, Pallas kernels: 2.1 us -> 1.38 us  [local(): pl.pallas_call(first_kernel, out_shape=[jax.ShapeDtypeStruct(face, f32),...]
    ppermute x1, starting transfers between devices: 1.63 us -> 1.9 us  [local(): got_even = lax.ppermute(even, 'gx', swap_even)]
where the time goes in v2:
time: 18.4 us; the launch traced here: 18.3 us
  starting transfers between devices  10.2 us (55%)
  waiting for transfers between devices  5 us (27%)
  Pallas kernels  2.38 us (13%)
  between operations  0.67 us (4%)
    ppermute x3, starting transfers between devices, shift(): lax.ppermute(value, 'gy', [(i, (i + by) % peers) for i in range(peers)])  4.76 us
    ppermute x1, starting transfers between devices, local(): got_odd = lax.ppermute(odd, 'gx', swap_odd)  3.55 us
    ppermute x1, waiting for transfers between devices, local(): got_odd = lax.ppermute(odd, 'gx', swap_odd)  3.19 us
    ppermute x1, starting transfers between devices, local(): got_even = lax.ppermute(even, 'gx', swap_even)  1.9 us
    ppermute x3, waiting for transfers between devices, shift(): lax.ppermute(value, 'gy', [(i, (i + by) % peers) for i in range(peers)])  1.81 us
    pallas_call x1, Pallas kernels, local(): pl.pallas_call(first_kernel, out_shape=[jax.ShapeDtypeStruct(face, f32),...  1.38 us
    pallas_call x1, Pallas kernels, local(): pl.pallas_call(lambda *refs: third_kernel(*refs, names=names), out_shape=...  0.81 us
  transfers between devices with their start and end apart: 5, of which 2 were waited for; matrix products, arithmetic and copies ran while one was open for 0% of the time, Pallas kernels for 0%

profile of v2, /device:TPU:0, one launch (start us, length us, event | category | flops | bytes accessed | tf_op | source)
XLA Modules:
  0.0 18.3 jit_solution(9127279280998324544)
XLA Ops:
  0.7 1.4 %first.1 = (f32[40,128]{1,0:T(8,128)S(1)}, f32[40,128]{1,0:T(8,128)S(1)}, f32[8,128]{1,0:T(8,128)S(1)}, f32[34,2,8,128]{3,2,1,0:T(8,128)S(1)}) custom-call(f32[27,2,8,128]{3,2,1,0:T(8,128)} %pop_h.1, f32[27]{0:T(128)} %relax_h.1, s32[2,8,128]{2,1,0:T(8,128)} %solid_h.1, s32[1,1,256]{2,1,0:T(1,128)} %cell_h.1, s32[1,1,256]{2,1,0:T(1,128)} %normal_h.1, ...), custom_call_target="tpu_custom_call" | custom-call | tf_op jit(solution)/shard_map/first/pallas_call | solution.py:341
  2.0 0.5 %collective-permute-start = (f32[40,128]{1,0:T(8,128)S(1)}, f32[40,128]{1,0:T(8,128)S(1)}, u32[]{:S(2)}, u32[]{:S(2)}) collective-permute-start(f32[40,128]{1,0:T(8,128)S(1)} %get-tuple-element.14), channel_id=1, source_target_pairs={{0,1},{1,2},{2,3},{3,0},{4,5},{5,6},{6,7},{7,4},{8,9},{9,10},{10,1... | collective-permute-start | bytes 61448 | tf_op jit(solution)/shard_map/ppermute | solution.py:375
  2.6 2.0 %collective-permute-start.1 = (f32[40,128]{1,0:T(8,128)S(1)}, f32[40,128]{1,0:T(8,128)S(1)}, u32[]{:S(2)}, u32[]{:S(2)}) collective-permute-start(f32[40,128]{1,0:T(8,128)S(1)} %get-tuple-element.15), channel_id=1, source_target_pairs={{0,3},{1,0},{2,1},{3,2},{4,7},{5,4},{6,5},{7,6},{8,11},{9,8},{10,9... | collective-permute-start | bytes 61448 | tf_op jit(solution)/shard_map/ppermute | solution.py:375
  4.6 2.2 %collective-permute-start.2 = (f32[8,128]{1,0:T(8,128)S(1)}, f32[8,128]{1,0:T(8,128)S(1)}, u32[]{:S(2)}, u32[]{:S(2)}) collective-permute-start(f32[8,128]{1,0:T(8,128)S(1)} %get-tuple-element.13.refs_0_), channel_id=1, source_target_pairs={{0,2},{1,3},{2,0},{3,1},{4,6},{5,7},{6,4},{7,5},{8,10},{9,11},{10,... | collective-permute-start | bytes 12296 | tf_op jit(solution)/shard_map/ppermute | solution.py:375
  6.8 1.8 %collective-permute-done.2.refs_4_ = f32[8,128]{1,0:T(8,128)S(1)} collective-permute-done((f32[8,128]{1,0:T(8,128)S(1)}, f32[8,128]{1,0:T(8,128)S(1)}, u32[]{:S(2)}, u32[]{:S(2)}) %collective-permute-start.2) | collective-permute-done | bytes 4128 | tf_op jit(solution)/shard_map/ppermute | solution.py:375
  8.6 0.0 collective-permute-done.refs_1_
  8.6 0.0 collective-permute-done.1.refs_2_
  8.6 0.2 %second.1 = (f32[27,2,8,128]{3,2,1,0:T(8,128)S(1)}, f32[40,128]{1,0:T(8,128)S(1)}, f32[11,8,128]{2,1,0:T(8,128)S(1)}, f32[11,8,128]{2,1,0:T(8,128)S(1)}) custom-call(f32[8,128]{1,0:T(8,128)S(1)} %get-tuple-element.13.refs_0_, f32[40,128]{1,0:T(8,128)S(1)} %collective-permute-done.refs_1_, f32[40,128]{1,0:T(8,128)S(1)} %collective-permute-done.1.refs_2_, ...), custom_call_target="tpu_custom_call" | custom-call | tf_op jit(solution)/shard_map/second/pallas_call | solution.py:381
  8.8 1.9 %collective-permute-start.3 = (f32[11,8,128]{2,1,0:T(8,128)S(1)}, f32[11,8,128]{2,1,0:T(8,128)S(1)}, u32[]{:S(2)}, u32[]{:S(2)}) collective-permute-start(f32[11,8,128]{2,1,0:T(8,128)S(1)} %get-tuple-element.19), channel_id=1, source_target_pairs={{0,4},{4,0},{8,12},{12,8},{16,20},{20,16},{24,28},{28,24},{1,5},{5... | collective-permute-start | bytes 135176 | tf_op jit(solution)/shard_map/ppermute | solution.py:398
  10.7 3.5 %collective-permute-start.4 = (f32[11,8,128]{2,1,0:T(8,128)S(1)}, f32[11,8,128]{2,1,0:T(8,128)S(1)}, u32[]{:S(2)}, u32[]{:S(2)}) collective-permute-start(f32[11,8,128]{2,1,0:T(8,128)S(1)} %get-tuple-element.20), channel_id=1, source_target_pairs={{0,28},{4,8},{8,4},{12,16},{16,12},{20,24},{24,20},{28,0},{1,29},{... | collective-permute-start | bytes 135176 | tf_op jit(solution)/shard_map/ppermute | solution.py:397
  14.3 0.0 collective-permute-done.3.refs_3_
  14.3 3.2 %collective-permute-done.4.refs_4_ = f32[11,8,128]{2,1,0:T(8,128)S(1)} collective-permute-done((f32[11,8,128]{2,1,0:T(8,128)S(1)}, f32[11,8,128]{2,1,0:T(8,128)S(1)}, u32[]{:S(2)}, u32[]{:S(2)}) %collective-permute-start.4) | collective-permute-done | bytes 45088 | tf_op jit(solution)/shard_map/ppermute | solution.py:397
  17.4 0.8 %third.1 = f32[27,2,8,128]{3,2,1,0:T(8,128)} custom-call(f32[27,2,8,128]{3,2,1,0:T(8,128)S(1)} %get-tuple-element.17.refs_0_, f32[40,128]{1,0:T(8,128)S(1)} %get-tuple-element.18.refs_1_, f32[34,2,8,128]{3,2,1,0:T(8,128)S(1)} %get-tuple-element.16.refs_3_.refs_2_, f32[11,8,128]{2,1,0:T(8,128)S(1)} %collective-permute-done.3.refs_3_, ...), custom_call_target="tpu_custom_call" | custom-call | tf_op jit(solution)/shard_map/third/pallas_call | solution.py:399
Async XLA Ops:
  2.0 6.6 %collective-permute-start = (f32[40,128]{1,0:T(8,128)S(1)}, f32[40,128]{1,0:T(8,128)S(1)}, u32[]{:S(2)}, u32[]{:S(2)}) collective-permute-start(f32[40,128]{1,0:T(8,128)S(1)} %get-tuple-element.14), channel_id=1, source_target_pairs={{0,1},{1,2},{2,3},{3,0},{4,5},{5,6},{6,7},{7,4},{8,9},{9,10},{10,1... | collective-permute-start | bytes 61448 | tf_op jit(solution)/shard_map/ppermute | solution.py:375
  2.6 6.0 %collective-permute-start.1 = (f32[40,128]{1,0:T(8,128)S(1)}, f32[40,128]{1,0:T(8,128)S(1)}, u32[]{:S(2)}, u32[]{:S(2)}) collective-permute-start(f32[40,128]{1,0:T(8,128)S(1)} %get-tuple-element.15), channel_id=1, source_target_pairs={{0,3},{1,0},{2,1},{3,2},{4,7},{5,4},{6,5},{7,6},{8,11},{9,8},{10,9... | collective-permute-start | bytes 61448 | tf_op jit(solution)/shard_map/ppermute | solution.py:375
  4.6 4.0 %collective-permute-start.2 = (f32[8,128]{1,0:T(8,128)S(1)}, f32[8,128]{1,0:T(8,128)S(1)}, u32[]{:S(2)}, u32[]{:S(2)}) collective-permute-start(f32[8,128]{1,0:T(8,128)S(1)} %get-tuple-element.13.refs_0_), channel_id=1, source_target_pairs={{0,2},{1,3},{2,0},{3,1},{4,6},{5,7},{6,4},{7,5},{8,10},{9,11},{10,... | collective-permute-start | bytes 12296 | tf_op jit(solution)/shard_map/ppermute | solution.py:375
  8.8 5.5 %collective-permute-start.3 = (f32[11,8,128]{2,1,0:T(8,128)S(1)}, f32[11,8,128]{2,1,0:T(8,128)S(1)}, u32[]{:S(2)}, u32[]{:S(2)}) collective-permute-start(f32[11,8,128]{2,1,0:T(8,128)S(1)} %get-tuple-element.19), channel_id=1, source_target_pairs={{0,4},{4,0},{8,12},{12,8},{16,20},{20,16},{24,28},{28,24},{1,5},{5... | collective-permute-start | bytes 135176 | tf_op jit(solution)/shard_map/ppermute | solution.py:398
  10.7 6.7 %collective-permute-start.4 = (f32[11,8,128]{2,1,0:T(8,128)S(1)}, f32[11,8,128]{2,1,0:T(8,128)S(1)}, u32[]{:S(2)}, u32[]{:S(2)}) collective-permute-start(f32[11,8,128]{2,1,0:T(8,128)S(1)} %get-tuple-element.20), channel_id=1, source_target_pairs={{0,28},{4,8},{8,4},{12,16},{16,12},{20,24},{24,20},{28,0},{1,29},{... | collective-permute-start | bytes 135176 | tf_op jit(solution)/shard_map/ppermute | solution.py:397

commit v3 on v2

--- a/solution.py
+++ b/solution.py
@@ -1,10 +1,10 @@
 import jax
 import jax.numpy as jnp
-import numpy as np
 from jax import lax
 from jax.experimental import pallas as pl
 from jax.experimental.pallas import tpu as pltpu
 from jax.sharding import PartitionSpec as P
+
 
 wall_ratio = (1.0 / 9.0) ** (1.0 / 7.0)
 LANES = 128
@@ -111,8 +111,8 @@
 
 def first_kernel(
     pop_h, relax_h, solid_h, cell_h, normal_h, count_h, ref_h, scell_h, sweight_h,
-    up_o, down_o, sample_o, state_o,
-    pop, relax, solid, cell, normal, count, ref, scell, sweight, sems,
+    even_o, odd_o, sample_o, state_o,
+    pop, relax, solid, cell, normal, count, ref, scell, sweight, sems, *, gy,
 ):
     size_x = pop.shape[1]
     walls, slots = cell.shape[1], scell.shape[1]
@@ -160,7 +160,7 @@
         for d in range(3):
             r = d * (slots // LANES) + t
             line = jnp.sum(total[d], axis=0, keepdims=True)
-            for o in (up_o, down_o, sample_o):
+            for o in (even_o, odd_o, sample_o):
                 o[r : r + 1, :] = line
     row, z = cell[...] // LANES, cell[...] % LANES
     live = lax.broadcasted_iota(jnp.int32, (1, walls), 1) < count[0, 0]
@@ -180,25 +180,29 @@
         state_o[REF, x] = ((high // 4) * LANES + low - 1).astype(jnp.float32)
         state_o[AXIS, x] = (high % 4).astype(jnp.float32)
     base = up(3 * (slots // LANES))
-    for o, b, y in ((up_o, 2, ROWS - 1), (down_o, 0, 0)):
+    parity = lax.axis_index(gy) % 2
+    faces = []
+    for b, y in ((2, ROWS - 1), (0, 0)):
         planes = [direction(a, b, c) for a in range(3) for c in range(3)] + list(range(RHO, PLANES))
-        for n, plane in enumerate(planes):
-            for x in range(size_x):
-                r = base + n * size_x + x
-                o[r : r + 1, :] = state_o[plane, x, y : y + 1, :]
-
-
-def second_kernel(own, from_below, from_above, *rest, names, peers, slots, slots_each):
+        faces.append([state_o[plane, x, y : y + 1, :] for plane in planes for x in range(size_x)])
+    for n, (above, below) in enumerate(zip(*faces)):
+        even_o[base + n : base + n + 1, :] = jnp.where(parity == 0, above, below)
+        odd_o[base + n : base + n + 1, :] = jnp.where(parity == 0, below, above)
+
+
+def second_kernel(own, y_even, y_odd, *rest, gy, peers, slots, slots_each):
     state, rest = rest[0], rest[1:]
     far, outs = rest[: peers - 3], rest[peers - 3 :]
-    post_o, edge_o, even_o, odd_o = outs
-    gx, gy = names
+    post_o, edge_o, plus_o, minus_o = outs
     size_x = post_o.shape[1]
     width = slots // LANES
     base = up(3 * width)
     me = lax.axis_index(gy)
-    parity = lax.axis_index(gx) % 2
-    tables = [(own, me), (from_below, (me + peers - 1) % peers), (from_above, (me + 1) % peers)]
+    below, above = (me + peers - 1) % peers, (me + 1) % peers
+    y_parity = me % 2
+    tables = [(own, me)]
+    tables.append((y_even, jnp.where(y_parity == 0, above, below)))
+    tables.append((y_odd, jnp.where(y_parity == 0, below, above)))
     for n, table in enumerate(far):
         tables.append((table, (me + peers - (n + 2)) % peers))
 
@@ -212,8 +216,8 @@
         for d in range(3):
             picked = jnp.zeros(ref.shape, jnp.float32)
             for table, who in tables:
-                line = table[pl.ds(d * width + tile, 1), :]
-                got = lanes_of(jnp.broadcast_to(line, (ROWS, LANES)), lane)
+                row = table[pl.ds(d * width + tile, 1), :]
+                got = lanes_of(jnp.broadcast_to(row, (ROWS, LANES)), lane)
                 picked = jnp.where(source == who, got, picked)
             tangential = jnp.where(axis == d, 0.0, wall_ratio * picked)
             out.append(jnp.where(ref >= 0, tangential, vel[d]))
@@ -235,11 +239,14 @@
     plus.append(state[SOLID, size_x - 1])
     minus.append(state[SOLID, 0])
     sub = lax.broadcasted_iota(jnp.int32, (ROWS, LANES), 0)
-    for side, (table, b, block) in enumerate(
-        ((from_below, 2, (me + peers - 1) % peers), (from_above, 0, (me + 1) % peers))
-    ):
+    for side, (b, block) in enumerate(((2, below), (0, above))):
+
+        def line(r):
+            got = (y_odd[r : r + 1, :], y_even[r : r + 1, :])
+            return jnp.where(y_parity == 0, got[side], got[1 - side])
+
         def plane(n):
-            rows = [table[base + n * size_x + x : base + n * size_x + x + 1, :] for x in range(size_x)]
+            rows = [line(base + n * size_x + x) for x in range(size_x)]
             tile = jnp.broadcast_to(rows[0], (ROWS, LANES))
             for x in range(1, size_x):
                 tile = jnp.where(sub == x, jnp.broadcast_to(rows[x], (ROWS, LANES)), tile)
@@ -264,26 +271,17 @@
         corner_plus.append(solid[size_x - 1 : size_x])
         corner_minus.append(solid[0:1])
     for n in range(10):
-        even_o[n] = jnp.where(parity == 0, plus[n], minus[n])
-        odd_o[n] = jnp.where(parity == 0, minus[n], plus[n])
+        plus_o[n] = plus[n]
+        minus_o[n] = minus[n]
     for n in range(8):
-        even_o[10, n : n + 1, :] = jnp.where(parity == 0, corner_plus[n], corner_minus[n])
-        odd_o[10, n : n + 1, :] = jnp.where(parity == 0, corner_minus[n], corner_plus[n])
-
-
-def third_kernel(post, edge, state, even, odd, out_h, out, sems, *, names):
-    gx, gy = names
+        plus_o[10, n : n + 1, :] = corner_plus[n]
+        minus_o[10, n : n + 1, :] = corner_minus[n]
+
+
+def third_kernel(post, edge, state, below, above, out_h, out, sems):
     size_x = post.shape[1]
-    parity = lax.axis_index(gx) % 2
     sub = lax.broadcasted_iota(jnp.int32, (ROWS, LANES), 0)
-
-    def below(n):
-        return jnp.where(parity == 0, odd[n], even[n])
-
-    def above(n):
-        return jnp.where(parity == 0, even[n], odd[n])
-
-    corners = {-1: below(10), size_x: above(10)}
+    corners = {-1: below[10], size_x: above[10]}
 
     def shifted(tile, row, step_y):
         if step_y == 0:
@@ -298,7 +296,7 @@
             r = (side * 10 + n_edge) * size_x + x
             row = edge[r : r + 1, :] if step_y else None
         else:
-            tile = below(n_face) if x < 0 else above(n_face)
+            tile = below[n_face] if x < 0 else above[n_face]
             row = corners[x][side * 4 + n_corner : side * 4 + n_corner + 1] if step_y else None
         return shifted(tile, row, step_y)
 
@@ -326,20 +324,20 @@
 def local(
     populations, relax, solid, wall_cell, wall_normal, wall_count, sample_ref, stencil_cell, stencil_weight
 ):
-    chans, size_x, size_y, size_z = populations.shape
+    _, size_x, size_y, size_z = populations.shape
     walls, slots = wall_cell.shape[-1], stencil_cell.shape[-1]
     devices, peers = lax.axis_size("gx"), lax.axis_size("gy")
     slots_each = slots // peers
     if (size_y, size_z) != (ROWS, LANES) or walls % LANES or slots % LANES:
         raise ValueError("unsupported block")
-    if LANES % slots_each or devices % 2 or peers < 4:
+    if LANES % slots_each or peers % 2 or peers < 4:
         raise ValueError("unsupported mesh")
     f32 = jnp.float32
     lines = up(3 * (slots // LANES))
     face = (lines + FACE * size_x, LANES)
     block = (size_x, ROWS, LANES)
-    up_face, down_face, samples, state = pl.pallas_call(
-        first_kernel,
+    y_even, y_odd, samples, state = pl.pallas_call(
+        lambda *refs: first_kernel(*refs, gy="gy"),
         out_shape=[
             jax.ShapeDtypeStruct(face, f32),
             jax.ShapeDtypeStruct(face, f32),
@@ -371,40 +369,38 @@
         )
     )
 
-    def shift(value, by):
-        return lax.ppermute(value, "gy", [(i, (i + by) % peers) for i in range(peers)])
-
-    from_below = shift(up_face, 1)
-    from_above = shift(down_face, peers - 1)
-    far = [shift(samples, n) for n in range(2, peers - 1)]
-    names = ("gx", "gy")
-    post, edge, even, odd = pl.pallas_call(
-        lambda *refs: second_kernel(*refs, names=names, peers=peers, slots=slots, slots_each=slots_each),
+    def swap(value, odd):
+        return lax.ppermute(value, "gy", [(i, (((i - odd) ^ 1) + odd) % peers) for i in range(peers)])
+
+    got_far = []
+    for n in range(2, peers - 1):
+        got_far.append(lax.ppermute(samples, "gy", [(i, (i + n) % peers) for i in range(peers)]))
+    y_odd = swap(y_odd, 1)
+    y_even = swap(y_even, 0)
+    post, edge, plus, minus = pl.pallas_call(
+        lambda *refs: second_kernel(*refs, gy="gy", peers=peers, slots=slots, slots_each=slots_each),
         out_shape=[
             jax.ShapeDtypeStruct(populations.shape, f32),
             jax.ShapeDtypeStruct((up(20 * size_x), LANES), f32),
             jax.ShapeDtypeStruct((11, ROWS, LANES), f32),
             jax.ShapeDtypeStruct((11, ROWS, LANES), f32),
         ],
-        in_specs=[VMEM] * (4 + len(far)),
+        in_specs=[VMEM] * (4 + len(got_far)),
         out_specs=[VMEM] * 4,
         compiler_params=pltpu.CompilerParams(vmem_limit_bytes=GRANT),
         name="second",
-    )(samples, from_below, from_above, state, *far)
-    swap_even = [(i, i ^ 1) for i in range(devices)]
-    swap_odd = [(i, ((i - 1) ^ 1) + 1) for i in range(devices)]
-    swap_odd = [(i, j % devices) for i, j in swap_odd]
-    got_odd = lax.ppermute(odd, "gx", swap_odd)
-    got_even = lax.ppermute(even, "gx", swap_even)
+    )(samples, y_even, y_odd, state, *got_far)
+    from_below = lax.ppermute(plus, "gx", [(i, (i + 1) % devices) for i in range(devices)])
+    from_above = lax.ppermute(minus, "gx", [(i, (i - 1) % devices) for i in range(devices)])
     return pl.pallas_call(
-        lambda *refs: third_kernel(*refs, names=names),
+        third_kernel,
         out_shape=jax.ShapeDtypeStruct(populations.shape, f32),
         in_specs=[VMEM] * 5,
         out_specs=HBM,
         scratch_shapes=[pltpu.VMEM(populations.shape, f32), pltpu.SemaphoreType.DMA((3,))],
         compiler_params=pltpu.CompilerParams(vmem_limit_bytes=GRANT),
         name="third",
-    )(post, edge, state, got_even, got_odd)
+    )(post, edge, state, from_below, from_above)
 
 
 def solution(mesh):

time: 18.4 us -> 16.8 us (0.913)
  starting transfers between devices: 10.2 us -> 7.96 us
  waiting for transfers between devices: 5 us -> 5.59 us
    ppermute x5, starting transfers between devices: 10.2 us -> 7.96 us  [the longest x1 3.2 us: local(): lax.ppermute(minus, 'gx', [(i, (i - 1) % devices) for i in range(devices)])]
    ppermute x5, waiting for transfers between devices: 5 us -> 5.59 us  [the longest x1 3.56 us: local(): lax.ppermute(samples, 'gy', [(i, (i + n) % peers) for i in range(peers)])]
where the time goes in v3:
time: 16.8 us; the launch traced here: 16.6 us
  starting transfers between devices  7.96 us (47%)
  waiting for transfers between devices  5.59 us (33%)
  Pallas kernels  2.38 us (14%)
  between operations  0.67 us (4%)
    ppermute x1, waiting for transfers between devices, local(): lax.ppermute(samples, 'gy', [(i, (i + n) % peers) for i in range(peers)])  3.56 us
    ppermute x1, starting transfers between devices, local(): lax.ppermute(minus, 'gx', [(i, (i - 1) % devices) for i in range(devices)])  3.2 us
    ppermute x2, starting transfers between devices, swap(): lax.ppermute(value, 'gy', [(i, ((i - odd ^ 1) + odd) % peers) for i in ra...  3.15 us
    ppermute x1, waiting for transfers between devices, local(): lax.ppermute(plus, 'gx', [(i, (i + 1) % devices) for i in range(devices)])  2.02 us
    ppermute x1, starting transfers between devices, local(): lax.ppermute(plus, 'gx', [(i, (i + 1) % devices) for i in range(devices)])  1.57 us
    pallas_call x1, Pallas kernels, local(): pl.pallas_call(lambda *refs: first_kernel(*refs, gy='gy'), out_shape=[jax...  1.38 us
    pallas_call x1, Pallas kernels, local(): pl.pallas_call(third_kernel, out_shape=jax.ShapeDtypeStruct(populations.s...  0.81 us
  transfers between devices with their start and end apart: 5, of which 2 were waited for; matrix products, arithmetic and copies ran while one was open for 0% of the time, Pallas kernels for 0%

profile of v3, /device:TPU:0, one launch (start us, length us, event | category | flops | bytes accessed | tf_op | source)
XLA Modules:
  0.0 16.6 jit_solution(9006186278773206036)
XLA Ops:
  0.7 1.4 %first.1 = (f32[40,128]{1,0:T(8,128)S(1)}, f32[40,128]{1,0:T(8,128)S(1)}, f32[8,128]{1,0:T(8,128)S(1)}, f32[34,2,8,128]{3,2,1,0:T(8,128)S(1)}) custom-call(f32[27,2,8,128]{3,2,1,0:T(8,128)} %refs_0_.1, f32[27]{0:T(128)} %refs_1_.1, s32[2,8,128]{2,1,0:T(8,128)} %refs_2_.1, s32[1,1,256]{2,1,0:T(1,128)} %refs_3_.1, s32[1,1,256]{2,1,0:T(1,128)} %refs_4_.1, ...), custom_call_target="tpu_custom_call" | custom-call | tf_op jit(solution)/shard_map/first/pallas_call | solution.py:339
  2.0 0.6 %collective-permute-start = (f32[40,128]{1,0:T(8,128)S(1)}, f32[40,128]{1,0:T(8,128)S(1)}, u32[]{:S(2)}, u32[]{:S(2)}) collective-permute-start(f32[40,128]{1,0:T(8,128)S(1)} %get-tuple-element.14), channel_id=1, source_target_pairs={{0,1},{1,0},{2,3},{3,2},{4,5},{5,4},{6,7},{7,6},{8,9},{9,8},{10,11... | collective-permute-start | bytes 61448 | tf_op jit(solution)/shard_map/ppermute | solution.py:373
  2.6 2.6 %collective-permute-start.1 = (f32[40,128]{1,0:T(8,128)S(1)}, f32[40,128]{1,0:T(8,128)S(1)}, u32[]{:S(2)}, u32[]{:S(2)}) collective-permute-start(f32[40,128]{1,0:T(8,128)S(1)} %get-tuple-element.15), channel_id=1, source_target_pairs={{0,3},{1,2},{2,1},{3,0},{4,7},{5,6},{6,5},{7,4},{8,11},{9,10},{10,... | collective-permute-start | bytes 61448 | tf_op jit(solution)/shard_map/ppermute | solution.py:373
  5.2 0.0 collective-permute-start.2
  5.2 3.6 %collective-permute-done.2.refs_4_ = f32[8,128]{1,0:T(8,128)S(1)} collective-permute-done((f32[8,128]{1,0:T(8,128)S(1)}, f32[8,128]{1,0:T(8,128)S(1)}, u32[]{:S(2)}, u32[]{:S(2)}) %collective-permute-start.2) | collective-permute-done | bytes 4128 | tf_op jit(solution)/shard_map/ppermute | solution.py:377
  8.8 0.0 collective-permute-done.refs_1_
  8.8 0.0 collective-permute-done.1.refs_2_
  8.8 0.2 %second.1 = (f32[27,2,8,128]{3,2,1,0:T(8,128)S(1)}, f32[40,128]{1,0:T(8,128)S(1)}, f32[11,8,128]{2,1,0:T(8,128)S(1)}, f32[11,8,128]{2,1,0:T(8,128)S(1)}) custom-call(f32[8,128]{1,0:T(8,128)S(1)} %get-tuple-element.13.refs_0_, f32[40,128]{1,0:T(8,128)S(1)} %collective-permute-done.refs_1_, f32[40,128]{1,0:T(8,128)S(1)} %collective-permute-done.1.refs_2_, ...), custom_call_target="tpu_custom_call" | custom-call | tf_op jit(solution)/shard_map/second/pallas_call | solution.py:380
  9.0 1.6 %collective-permute-start.3 = (f32[11,8,128]{2,1,0:T(8,128)S(1)}, f32[11,8,128]{2,1,0:T(8,128)S(1)}, u32[]{:S(2)}, u32[]{:S(2)}) collective-permute-start(f32[11,8,128]{2,1,0:T(8,128)S(1)} %get-tuple-element.19), channel_id=1, source_target_pairs={{0,4},{4,8},{8,12},{12,16},{16,20},{20,24},{24,28},{28,0},{1,5},{5... | collective-permute-start | bytes 135176 | tf_op jit(solution)/shard_map/ppermute | solution.py:393
  10.6 3.2 %collective-permute-start.4 = (f32[11,8,128]{2,1,0:T(8,128)S(1)}, f32[11,8,128]{2,1,0:T(8,128)S(1)}, u32[]{:S(2)}, u32[]{:S(2)}) collective-permute-start(f32[11,8,128]{2,1,0:T(8,128)S(1)} %get-tuple-element.20), channel_id=1, source_target_pairs={{0,28},{4,0},{8,4},{12,8},{16,12},{20,16},{24,20},{28,24},{1,29},{... | collective-permute-start | bytes 135176 | tf_op jit(solution)/shard_map/ppermute | solution.py:394
  13.8 2.0 %collective-permute-done.3.below = f32[11,8,128]{2,1,0:T(8,128)S(1)} collective-permute-done((f32[11,8,128]{2,1,0:T(8,128)S(1)}, f32[11,8,128]{2,1,0:T(8,128)S(1)}, u32[]{:S(2)}, u32[]{:S(2)}) %collective-permute-start.3) | collective-permute-done | bytes 45088 | tf_op jit(solution)/shard_map/ppermute | solution.py:393
  15.8 0.0 collective-permute-done.4.above
  15.8 0.8 %third.1 = f32[27,2,8,128]{3,2,1,0:T(8,128)} custom-call(f32[27,2,8,128]{3,2,1,0:T(8,128)S(1)} %get-tuple-element.17.post, f32[40,128]{1,0:T(8,128)S(1)} %get-tuple-element.18.edge, f32[34,2,8,128]{3,2,1,0:T(8,128)S(1)} %get-tuple-element.16.refs_3_.state, f32[11,8,128]{2,1,0:T(8,128)S(1)} %collective-permute-done.3.below, ...), custom_call_target="tpu_custom_call" | custom-call | tf_op jit(solution)/shard_map/third/pallas_call | solution.py:395
Async XLA Ops:
  2.0 6.8 %collective-permute-start = (f32[40,128]{1,0:T(8,128)S(1)}, f32[40,128]{1,0:T(8,128)S(1)}, u32[]{:S(2)}, u32[]{:S(2)}) collective-permute-start(f32[40,128]{1,0:T(8,128)S(1)} %get-tuple-element.14), channel_id=1, source_target_pairs={{0,1},{1,0},{2,3},{3,2},{4,5},{5,4},{6,7},{7,6},{8,9},{9,8},{10,11... | collective-permute-start | bytes 61448 | tf_op jit(solution)/shard_map/ppermute | solution.py:373
  2.6 6.2 %collective-permute-start.1 = (f32[40,128]{1,0:T(8,128)S(1)}, f32[40,128]{1,0:T(8,128)S(1)}, u32[]{:S(2)}, u32[]{:S(2)}) collective-permute-start(f32[40,128]{1,0:T(8,128)S(1)} %get-tuple-element.15), channel_id=1, source_target_pairs={{0,3},{1,2},{2,1},{3,0},{4,7},{5,6},{6,5},{7,4},{8,11},{9,10},{10,... | collective-permute-start | bytes 61448 | tf_op jit(solution)/shard_map/ppermute | solution.py:373
  5.2 3.6 %collective-permute-start.2 = (f32[8,128]{1,0:T(8,128)S(1)}, f32[8,128]{1,0:T(8,128)S(1)}, u32[]{:S(2)}, u32[]{:S(2)}) collective-permute-start(f32[8,128]{1,0:T(8,128)S(1)} %get-tuple-element.13.refs_0_), channel_id=1, source_target_pairs={{0,2},{1,3},{2,0},{3,1},{4,6},{5,7},{6,4},{7,5},{8,10},{9,11},{10,... | collective-permute-start | bytes 12296 | tf_op jit(solution)/shard_map/ppermute | solution.py:377
  9.0 6.8 %collective-permute-start.3 = (f32[11,8,128]{2,1,0:T(8,128)S(1)}, f32[11,8,128]{2,1,0:T(8,128)S(1)}, u32[]{:S(2)}, u32[]{:S(2)}) collective-permute-start(f32[11,8,128]{2,1,0:T(8,128)S(1)} %get-tuple-element.19), channel_id=1, source_target_pairs={{0,4},{4,8},{8,12},{12,16},{16,20},{20,24},{24,28},{28,0},{1,5},{5... | collective-permute-start | bytes 135176 | tf_op jit(solution)/shard_map/ppermute | solution.py:393
  10.6 5.2 %collective-permute-start.4 = (f32[11,8,128]{2,1,0:T(8,128)S(1)}, f32[11,8,128]{2,1,0:T(8,128)S(1)}, u32[]{:S(2)}, u32[]{:S(2)}) collective-permute-start(f32[11,8,128]{2,1,0:T(8,128)S(1)} %get-tuple-element.20), channel_id=1, source_target_pairs={{0,28},{4,0},{8,4},{12,8},{16,12},{20,16},{24,20},{28,24},{1,29},{... | collective-permute-start | bytes 135176 | tf_op jit(solution)/shard_map/ppermute | solution.py:394

commit v4 on v3

--- a/solution.py
+++ b/solution.py
@@ -9,10 +9,12 @@
 wall_ratio = (1.0 / 9.0) ** (1.0 / 7.0)
 LANES = 128
 ROWS = 8
-RHO, VEL, REF, AXIS, SOLID, PLANES = 27, 28, 31, 32, 33, 34
+RHO, VEL, PLANES = 27, 28, 31
+REF, AXIS, SOLID = 0, 1, 2
 FACE = 16
 HBM = pl.BlockSpec(memory_space=pltpu.HBM)
 VMEM = pl.BlockSpec(memory_space=pltpu.VMEM)
+COVER = 4 * 10**9
 GRANT = 4 * 1024 * 1024
 
 
@@ -59,7 +61,7 @@
     return values
 
 
-def relaxed(pops, relax):
+def relaxed(pops, keep):
     single = (1.0 / 6.0, 2.0 / 3.0, 1.0 / 6.0)
     weight = [single[i // 9] * single[i // 3 % 3] * single[i % 3] for i in range(27)]
 
@@ -98,7 +100,7 @@
                 t = t if abs(f - 1.0) < 1e-12 else f * t
                 eq = t if eq is None else eq + t
         dev = moment[i] if eq is None else moment[i] - eq
-        kept.append((1.0 - relax[i]) * dev)
+        kept.append(keep[i] * dev)
     back = (3.0, 1.5, 3.0)
     kept = along_axes(kept, undo)
     kept = [back[i // 9] * back[i // 3 % 3] * back[i % 3] * k for i, k in enumerate(kept)]
@@ -109,23 +111,20 @@
     return jnp.take_along_axis(table, index, axis=1, mode="promise_in_bounds")
 
 
-def first_kernel(
-    pop_h, relax_h, solid_h, cell_h, normal_h, count_h, ref_h, scell_h, sweight_h,
-    even_o, odd_o, sample_o, state_o,
-    pop, relax, solid, cell, normal, count, ref, scell, sweight, sems, *, gy,
-):
-    size_x = pop.shape[1]
-    walls, slots = cell.shape[1], scell.shape[1]
-    moves = [
-        (relax_h, relax), (count_h, count), (scell_h.at[0, 0], scell), (sweight_h.at[0, 0], sweight),
-        (cell_h.at[0], cell), (normal_h.at[0], normal), (ref_h.at[0], ref), (pop_h, pop), (solid_h, solid),
-    ]
-    copies = [pltpu.make_async_copy(s, d, sems.at[n]) for n, (s, d) in enumerate(moves)]
-    for copy in copies:
-        copy.start()
-    for copy in copies:
-        copy.wait()
-    rates = [relax[i] for i in range(27)]
+def number_kernel(out):
+    out[...] = lax.broadcasted_iota(jnp.int32, out.shape, 1)
+
+
+def live_kernel(number, cell, normal, ref, relax, count, cell_o, axis_o, ref_o, keep_o):
+    cell_o[...] = jnp.where(number[...] < count[0, 0], cell[0], -1)
+    axis_o[...] = normal[0] // 2
+    ref_o[...] = ref[0]
+    keep_o[...] = 1.0 - relax[...]
+
+
+def cell_kernel(keep, pop, scell, sweight, state_o, sample_o):
+    size_x, slots = pop.shape[1], scell.shape[-1]
+    rates = [jnp.broadcast_to(keep[0:1, i : i + 1], (ROWS, LANES)) for i in range(27)]
     velocity = []
     for x in range(size_x):
         density, vel, kept = relaxed([pop[i, x] for i in range(27)], rates)
@@ -135,11 +134,10 @@
         state_o[RHO, x] = density
         for d in range(3):
             state_o[VEL + d, x] = vel[d]
-        state_o[SOLID, x] = solid[x].astype(jnp.float32)
     sub = lax.broadcasted_iota(jnp.int32, (ROWS, LANES), 0)
     for t in range(slots // LANES):
-        cells = scell[:, t * LANES : (t + 1) * LANES]
-        weights = sweight[:, t * LANES : (t + 1) * LANES]
+        cells = scell[0, 0, :, t * LANES : (t + 1) * LANES]
+        weights = sweight[0, 0, :, t * LANES : (t + 1) * LANES]
         row, z = cells // LANES, cells % LANES
         low = jnp.broadcast_to(z[0:1], (ROWS, LANES))
         other = z != low
@@ -147,7 +145,7 @@
         high = jnp.broadcast_to(high, (ROWS, LANES))
         w_high = jnp.where(other, weights, 0.0)
         w_low = weights - w_high
-        total = [jnp.zeros((ROWS, LANES), jnp.float32) for _ in range(3)]
+        total = [None] * 3
         for x in range(size_x):
             a_low = jnp.zeros((ROWS, LANES), jnp.float32)
             a_high = a_low
@@ -156,16 +154,19 @@
                 a_low += jnp.where(hit, jnp.broadcast_to(w_low[k : k + 1], (ROWS, LANES)), 0.0)
                 a_high += jnp.where(hit, jnp.broadcast_to(w_high[k : k + 1], (ROWS, LANES)), 0.0)
             for d in range(3):
-                total[d] += a_low * lanes_of(velocity[x][d], low) + a_high * lanes_of(velocity[x][d], high)
+                part = a_low * lanes_of(velocity[x][d], low) + a_high * lanes_of(velocity[x][d], high)
+                total[d] = part if total[d] is None else total[d] + part
         for d in range(3):
             r = d * (slots // LANES) + t
-            line = jnp.sum(total[d], axis=0, keepdims=True)
-            for o in (even_o, odd_o, sample_o):
-                o[r : r + 1, :] = line
-    row, z = cell[...] // LANES, cell[...] % LANES
-    live = lax.broadcasted_iota(jnp.int32, (1, walls), 1) < count[0, 0]
-    low = jnp.where(live, ref[...] % LANES + 1, 0).astype(jnp.float32)
-    high = jnp.where(live, ref[...] // LANES * 4 + normal[...] // 2, 0).astype(jnp.float32)
+            sample_o[r : r + 1, :] = jnp.sum(total[d], axis=0, keepdims=True)
+
+
+def face_kernel(cell, axis, ref, solid, state, sample, even_o, odd_o, early_o, map_o, *, gy):
+    size_x, walls = solid.shape[0], cell.shape[-1]
+    row = jnp.where(cell[...] < 0, -1, cell[...] // LANES)
+    z = cell[...] % LANES
+    low = (ref[...] % LANES + 1).astype(jnp.float32)
+    high = (ref[...] // LANES * 4 + axis[...]).astype(jnp.float32)
     height = size_x * ROWS
     at = lax.broadcasted_iota(jnp.int32, (height, walls), 0) == jnp.broadcast_to(row, (height, walls))
     left = jnp.concatenate(
@@ -177,21 +178,29 @@
     for x in range(size_x):
         low = dense[x * ROWS : (x + 1) * ROWS].astype(jnp.int32)
         high = dense[height + x * ROWS : height + (x + 1) * ROWS].astype(jnp.int32)
-        state_o[REF, x] = ((high // 4) * LANES + low - 1).astype(jnp.float32)
-        state_o[AXIS, x] = (high % 4).astype(jnp.float32)
-    base = up(3 * (slots // LANES))
+        map_o[REF, x] = ((high // 4) * LANES + low - 1).astype(jnp.float32)
+        map_o[AXIS, x] = (high % 4).astype(jnp.float32)
+        map_o[SOLID, x] = solid[x].astype(jnp.float32)
+    for n in range(9):
+        early_o[n] = state[18 + n, size_x - 1]
+    early_o[9] = state[RHO, size_x - 1]
+    early_o[10] = map_o[SOLID, size_x - 1]
+    base = sample.shape[0]
+    even_o[:base, :] = sample[...]
+    odd_o[:base, :] = sample[...]
     parity = lax.axis_index(gy) % 2
     faces = []
     for b, y in ((2, ROWS - 1), (0, 0)):
-        planes = [direction(a, b, c) for a in range(3) for c in range(3)] + list(range(RHO, PLANES))
-        faces.append([state_o[plane, x, y : y + 1, :] for plane in planes for x in range(size_x)])
+        planes = [(state, direction(a, b, c)) for a in range(3) for c in range(3)]
+        planes += [(state, n) for n in range(RHO, PLANES)] + [(map_o, n) for n in range(3)]
+        faces.append([array[plane, x, y : y + 1, :] for array, plane in planes for x in range(size_x)])
     for n, (above, below) in enumerate(zip(*faces)):
         even_o[base + n : base + n + 1, :] = jnp.where(parity == 0, above, below)
         odd_o[base + n : base + n + 1, :] = jnp.where(parity == 0, below, above)
 
 
 def second_kernel(own, y_even, y_odd, *rest, gy, peers, slots, slots_each):
-    state, rest = rest[0], rest[1:]
+    state, maps, rest = rest[0], rest[1], rest[2:]
     far, outs = rest[: peers - 3], rest[peers - 3 :]
     post_o, edge_o, plus_o, minus_o = outs
     size_x = post_o.shape[1]
@@ -223,21 +232,21 @@
             out.append(jnp.where(ref >= 0, tangential, vel[d]))
         return out
 
-    plus, minus, corner_plus, corner_minus = [], [], [], []
+    minus, corner_plus, corner_minus = [], [], []
     for x in range(size_x):
-        ref = state[REF, x].astype(jnp.int32)
-        axis = state[AXIS, x].astype(jnp.int32)
+        ref = maps[REF, x].astype(jnp.int32)
+        axis = maps[AXIS, x].astype(jnp.int32)
         vel = walled(me, ref, axis, [state[VEL + d, x] for d in range(3)])
+        if x == size_x - 1:
+            for d in range(3):
+                plus_o[d] = vel[d]
         eq = equilibria(state[RHO, x], vel, range(27))
         for i in range(27):
             value = state[i, x] + eq[i]
             post_o[i, x] = value
-            if x == size_x - 1 and i >= 18:
-                plus.append(value)
             if x == 0 and i < 9:
                 minus.append(value)
-    plus.append(state[SOLID, size_x - 1])
-    minus.append(state[SOLID, 0])
+    minus.append(maps[SOLID, 0])
     sub = lax.broadcasted_iota(jnp.int32, (ROWS, LANES), 0)
     for side, (b, block) in enumerate(((2, below), (0, above))):
 
@@ -271,50 +280,70 @@
         corner_plus.append(solid[size_x - 1 : size_x])
         corner_minus.append(solid[0:1])
     for n in range(10):
-        plus_o[n] = plus[n]
         minus_o[n] = minus[n]
     for n in range(8):
-        plus_o[10, n : n + 1, :] = corner_plus[n]
+        plus_o[3, n : n + 1, :] = corner_plus[n]
         minus_o[10, n : n + 1, :] = corner_minus[n]
 
 
-def third_kernel(post, edge, state, below, above, out_h, out, sems):
+def shifted(tile, row, step_y):
+    if step_y == 0:
+        return tile
+    sub = lax.broadcasted_iota(jnp.int32, (ROWS, LANES), 0)
+    rolled = pltpu.roll(tile, step_y % ROWS, 0)
+    return jnp.where(sub == (0 if step_y > 0 else ROWS - 1), jnp.broadcast_to(row, (ROWS, LANES)), rolled)
+
+
+def along_z(tile, c):
+    return tile if c == 1 else pltpu.roll(tile, (c - 1) % LANES, 1)
+
+
+def inner_kernel(post, edge, maps, out_h, out, sems):
     size_x = post.shape[1]
-    sub = lax.broadcasted_iota(jnp.int32, (ROWS, LANES), 0)
-    corners = {-1: below[10], size_x: above[10]}
-
-    def shifted(tile, row, step_y):
-        if step_y == 0:
-            return tile
-        rolled = pltpu.roll(tile, step_y % ROWS, 0)
-        return jnp.where(sub == (0 if step_y > 0 else ROWS - 1), jnp.broadcast_to(row, (ROWS, LANES)), rolled)
-
-    def source(x, step_y, n_face, n_edge, n_corner, inside):
-        side = 0 if step_y > 0 else 1
-        if 0 <= x < size_x:
-            tile = inside(x)
-            r = (side * 10 + n_edge) * size_x + x
-            row = edge[r : r + 1, :] if step_y else None
-        else:
-            tile = below[n_face] if x < 0 else above[n_face]
-            row = corners[x][side * 4 + n_corner : side * 4 + n_corner + 1] if step_y else None
-        return shifted(tile, row, step_y)
-
     copies = []
-    for a in range(3):
+    for a in (1, 2, 0):
+        first, last = max(a - 1, 0), size_x + min(a - 1, 0)
         for b in range(3):
-            for x in range(size_x):
-                from_x, step_y = x - (a - 1), b - 1
-                wall = source(from_x, step_y, 9, 9, 3, lambda q: state[SOLID, q])
+            side = 0 if b == 2 else 1
+            for x in range(first, last):
+                q = x - (a - 1)
+
+                def row(n):
+                    r = (side * 10 + n) * size_x + q
+                    return edge[r : r + 1, :]
+
+                wall = shifted(maps[SOLID, q], row(9), b - 1)
                 for c in range(3):
                     i = direction(a, b, c)
-                    moved = source(from_x, step_y, 3 * b + c, 3 * a + c, c, lambda q: post[i, q])
-                    solid = wall
-                    if c != 1:
-                        moved = pltpu.roll(moved, (c - 1) % LANES, 1)
-                        solid = pltpu.roll(wall, (c - 1) % LANES, 1)
-                    out[i, x] = jnp.where(solid > 0.5, post[26 - i, x], moved)
-        copy = pltpu.make_async_copy(out.at[pl.ds(9 * a, 9)], out_h.at[pl.ds(9 * a, 9)], sems.at[a])
+                    moved = along_z(shifted(post[i, q], row(3 * a + c), b - 1), c)
+                    out[i, x] = jnp.where(along_z(wall, c) > 0.5, post[26 - i, x], moved)
+        part = (pl.ds(9 * a, 9), pl.ds(first, last - first))
+        copy = pltpu.make_async_copy(out.at[part], out_h.at[part], sems.at[a])
+        copy.start()
+        copies.append(copy)
+    for copy in copies:
+        copy.wait()
+
+
+def outer_kernel(post, early, below, above, held_h, out_h, out, sems):
+    del held_h
+    size_x = post.shape[1]
+    copies = []
+    for a, x in ((0, size_x - 1), (2, 0)):
+        if a == 0:
+            tiles, solid, corner = [above[n] for n in range(9)], above[9], above[10]
+        else:
+            eq = equilibria(early[9], [below[d] for d in range(3)], range(18, 27))
+            tiles, solid, corner = [early[n] + eq[18 + n] for n in range(9)], early[10], below[3]
+        for b in range(3):
+            side = 0 if b == 2 else 1
+            wall = shifted(solid, corner[side * 4 + 3 : side * 4 + 4], b - 1)
+            for c in range(3):
+                i = direction(a, b, c)
+                moved = shifted(tiles[3 * b + c], corner[side * 4 + c : side * 4 + c + 1], b - 1)
+                moved = along_z(moved, c)
+                out[i % 9 + 9 * (a // 2)] = jnp.where(along_z(wall, c) > 0.5, post[26 - i, x], moved)
+        copy = pltpu.make_async_copy(out.at[pl.ds(9 * (a // 2), 9)], out_h.at[pl.ds(9 * a, 9), x], sems.at[a // 2])
         copy.start()
         copies.append(copy)
     for copy in copies:
@@ -336,38 +365,44 @@
     lines = up(3 * (slots // LANES))
     face = (lines + FACE * size_x, LANES)
     block = (size_x, ROWS, LANES)
-    y_even, y_odd, samples, state = pl.pallas_call(
-        lambda *refs: first_kernel(*refs, gy="gy"),
+    number = pl.pallas_call(
+        number_kernel,
+        out_shape=jax.ShapeDtypeStruct((1, walls), jnp.int32),
+        out_specs=VMEM,
+        cost_estimate=pl.CostEstimate(flops=COVER, bytes_accessed=0, transcendentals=0),
+        compiler_params=pltpu.CompilerParams(vmem_limit_bytes=GRANT),
+        name="number",
+    )()
+    wall_row = jax.ShapeDtypeStruct((1, walls), jnp.int32)
+    cells, axis, refs, keep = pl.pallas_call(
+        live_kernel,
+        out_shape=[wall_row, wall_row, wall_row, jax.ShapeDtypeStruct((1, 27), f32)],
+        in_specs=[VMEM] * 5 + [pl.BlockSpec(memory_space=pltpu.SMEM)],
+        out_specs=[VMEM] * 4,
+        compiler_params=pltpu.CompilerParams(vmem_limit_bytes=GRANT),
+        name="live",
+    )(number, wall_cell, wall_normal, sample_ref, relax.reshape(1, 27), wall_count)
+    state, samples = pl.pallas_call(
+        cell_kernel,
+        out_shape=[jax.ShapeDtypeStruct((PLANES, *block), f32), jax.ShapeDtypeStruct((lines, LANES), f32)],
+        in_specs=[VMEM] * 4,
+        out_specs=[VMEM] * 2,
+        compiler_params=pltpu.CompilerParams(vmem_limit_bytes=GRANT),
+        name="cells",
+    )(keep, populations, stencil_cell, stencil_weight)
+    y_even, y_odd, early, maps = pl.pallas_call(
+        lambda *refs: face_kernel(*refs, gy="gy"),
         out_shape=[
             jax.ShapeDtypeStruct(face, f32),
             jax.ShapeDtypeStruct(face, f32),
-            jax.ShapeDtypeStruct((lines, LANES), f32),
-            jax.ShapeDtypeStruct((PLANES, *block), f32),
+            jax.ShapeDtypeStruct((11, ROWS, LANES), f32),
+            jax.ShapeDtypeStruct((3, *block), f32),
         ],
-        in_specs=[HBM] * 9,
+        in_specs=[VMEM] * 6,
         out_specs=[VMEM] * 4,
-        scratch_shapes=[
-            pltpu.VMEM(populations.shape, f32),
-            pltpu.SMEM(relax.shape, f32),
-            pltpu.VMEM(block, jnp.int32),
-            pltpu.VMEM((1, walls), jnp.int32),
-            pltpu.VMEM((1, walls), jnp.int32),
-            pltpu.SMEM((1, 1), jnp.int32),
-            pltpu.VMEM((1, walls), jnp.int32),
-            pltpu.VMEM((8, slots), jnp.int32),
-            pltpu.VMEM((8, slots), f32),
-            pltpu.SemaphoreType.DMA((9,)),
-        ],
-        compiler_params=pltpu.CompilerParams(vmem_limit_bytes=GRANT),
-        name="first",
-    )(
-        *(
-            v if v is wall_count else pltpu.with_memory_space_constraint(v, pltpu.HBM)
-            for v in (
-                populations, relax, solid, wall_cell, wall_normal, wall_count, sample_ref, stencil_cell, stencil_weight
-            )
-        )
-    )
+        compiler_params=pltpu.CompilerParams(vmem_limit_bytes=GRANT),
+        name="face",
+    )(cells, axis, refs, solid, state, samples)
 
     def swap(value, odd):
         return lax.ppermute(value, "gy", [(i, (((i - odd) ^ 1) + odd) % peers) for i in range(peers)])
@@ -377,30 +412,42 @@
         got_far.append(lax.ppermute(samples, "gy", [(i, (i + n) % peers) for i in range(peers)]))
     y_odd = swap(y_odd, 1)
     y_even = swap(y_even, 0)
+    ring = [(i, (i + 1) % devices) for i in range(devices)]
+    early = lax.ppermute(early, "gx", ring)
     post, edge, plus, minus = pl.pallas_call(
         lambda *refs: second_kernel(*refs, gy="gy", peers=peers, slots=slots, slots_each=slots_each),
         out_shape=[
             jax.ShapeDtypeStruct(populations.shape, f32),
             jax.ShapeDtypeStruct((up(20 * size_x), LANES), f32),
-            jax.ShapeDtypeStruct((11, ROWS, LANES), f32),
+            jax.ShapeDtypeStruct((4, ROWS, LANES), f32),
             jax.ShapeDtypeStruct((11, ROWS, LANES), f32),
         ],
-        in_specs=[VMEM] * (4 + len(got_far)),
+        in_specs=[VMEM] * (5 + len(got_far)),
         out_specs=[VMEM] * 4,
         compiler_params=pltpu.CompilerParams(vmem_limit_bytes=GRANT),
         name="second",
-    )(samples, y_even, y_odd, state, *got_far)
-    from_below = lax.ppermute(plus, "gx", [(i, (i + 1) % devices) for i in range(devices)])
+    )(samples, y_even, y_odd, state, maps, *got_far)
+    from_below = lax.ppermute(plus, "gx", ring)
     from_above = lax.ppermute(minus, "gx", [(i, (i - 1) % devices) for i in range(devices)])
-    return pl.pallas_call(
-        third_kernel,
+    held = pl.pallas_call(
+        inner_kernel,
         out_shape=jax.ShapeDtypeStruct(populations.shape, f32),
-        in_specs=[VMEM] * 5,
+        in_specs=[VMEM] * 3,
         out_specs=HBM,
         scratch_shapes=[pltpu.VMEM(populations.shape, f32), pltpu.SemaphoreType.DMA((3,))],
         compiler_params=pltpu.CompilerParams(vmem_limit_bytes=GRANT),
-        name="third",
-    )(post, edge, state, from_below, from_above)
+        name="inner",
+    )(post, edge, maps)
+    return pl.pallas_call(
+        outer_kernel,
+        out_shape=jax.ShapeDtypeStruct(populations.shape, f32),
+        in_specs=[VMEM] * 4 + [HBM],
+        out_specs=HBM,
+        input_output_aliases={4: 0},
+        scratch_shapes=[pltpu.VMEM((18, ROWS, LANES), f32), pltpu.SemaphoreType.DMA((2,))],
+        compiler_params=pltpu.CompilerParams(vmem_limit_bytes=GRANT),
+        name="outer",
+    )(post, early, from_below, from_above, pltpu.with_memory_space_constraint(held, pltpu.HBM))
 
 
 def solution(mesh):

time: 16.8 us -> 21 us (1.25)
  starting transfers between devices: 7.96 us -> 9.8 us
  waiting for transfers between devices: 5.59 us -> 7.21 us
  local copies, waits for them, and re-layouts: 0 us -> 0.85 us
  Pallas kernels: 2.38 us -> 2.09 us
    ppermute x1 -> x2, waiting for transfers between devices: 2.02 us -> 5.65 us  [the longest x1 5.65 us: local(): from_below = lax.ppermute(plus, 'gx', ring)]
    ppermute x1, waiting for transfers between devices: 3.56 us -> 1.55 us  [local(): lax.ppermute(samples, 'gy', [(i, (i + n) % peers) for i in range(peers)])]
    ppermute x1, starting transfers between devices: 3.2 us -> 4.61 us  [local(): lax.ppermute(minus, 'gx', [(i, (i - 1) % devices) for i in range(devices)])]
    unnamed x0 -> x16, local copies, waits for them, and re-layouts: none -> 0.85 us
    ppermute x1 -> x2, starting transfers between devices: 1.57 us -> 2.01 us  [the longest x1 2.01 us: local(): early = lax.ppermute(early, 'gx', ring)]
    pallas_call x2 -> x6, Pallas kernels: 2.19 us -> 1.9 us  [the longest x1 0.78 us: local(): pl.pallas_call(inner_kernel, out_shape=jax.ShapeDtypeStruct(populations.s...]
  transfers between devices with their start and end apart: 5 -> 6, of which waited for: 2 -> 2; matrix products, arithmetic and copies ran while one was open for 0% -> 0% of each run, Pallas kernels for 0% -> 5%
where the time goes in v4:
time: 21 us; the launch traced here: 20.8 us
  starting transfers between devices  9.8 us (47%)
  waiting for transfers between devices  7.21 us (34%)
  Pallas kernels  2.09 us (10%)
  between operations  0.87 us (4%)
  local copies, waits for them, and re-layouts  0.85 us (4%)
    ppermute x1, waiting for transfers between devices, local(): from_below = lax.ppermute(plus, 'gx', ring)  5.65 us
    ppermute x1, starting transfers between devices, local(): lax.ppermute(minus, 'gx', [(i, (i - 1) % devices) for i in range(devices)])  4.61 us
    ppermute x2, starting transfers between devices, swap(): lax.ppermute(value, 'gy', [(i, ((i - odd ^ 1) + odd) % peers) for i in ra...  3.13 us
    ppermute x1, starting transfers between devices, local(): early = lax.ppermute(early, 'gx', ring)  2.01 us
    ppermute x1, waiting for transfers between devices, local(): lax.ppermute(samples, 'gy', [(i, (i + n) % peers) for i in range(peers)])  1.55 us
    unnamed x16, local copies, waits for them, and re-layouts  0.85 us
    pallas_call x1, Pallas kernels, local(): pl.pallas_call(inner_kernel, out_shape=jax.ShapeDtypeStruct(populations.s...  0.78 us
    pallas_call x1, Pallas kernels, local(): pl.pallas_call(outer_kernel, out_shape=jax.ShapeDtypeStruct(populations.s...  0.73 us
  transfers between devices with their start and end apart: 6, of which 2 were waited for; matrix products, arithmetic and copies ran while one was open for 0% of the time, Pallas kernels for 5%

profile of v4, /device:TPU:0, one launch (start us, length us, event | category | flops | bytes accessed | tf_op | source)
XLA Modules:
  0.0 20.8 jit_solution(7376335019739789015)
XLA Ops:
  0.0 0.0 copy-start
  0.0 0.0 copy-start.4
  0.0 0.0 copy-start.5
  0.0 0.0 copy-start.6
  0.0 0.0 copy-start.3
  0.0 0.0 copy-start.2
  0.8 0.0 copy-done.4
  0.8 0.0 copy-done.5
  0.8 0.0 copy-done.6
  0.9 0.0 copy-done.7
  0.9 0.1 copy-done
  1.0 0.0 copy-done.3
  1.0 0.0 copy-done.2
  1.0 0.2 cells.1
  1.2 0.0 copy-start.1
  1.2 0.7 %copy-done.1 = s32[2,8,128]{2,1,0:T(8,128)S(1)} copy-done((s32[2,8,128]{2,1,0:T(8,128)S(1)}, s32[2,8,128]{2,1,0:T(8,128)}, u32[]{:S(2)}) %copy-start.1) | copy-done | bytes 8216
  1.9 0.2 face.1
  2.1 0.5 %collective-permute-start = (f32[40,128]{1,0:T(8,128)S(1)}, f32[40,128]{1,0:T(8,128)S(1)}, u32[]{:S(2)}, u32[]{:S(2)}) collective-permute-start(f32[40,128]{1,0:T(8,128)S(1)} %get-tuple-element.25), channel_id=1, source_target_pairs={{0,1},{1,0},{2,3},{3,2},{4,5},{5,4},{6,7},{7,6},{8,9},{9,8},{10,11... | collective-permute-start | bytes 61448 | tf_op jit(solution)/shard_map/ppermute | solution.py:408
  2.6 2.6 %collective-permute-start.1 = (f32[40,128]{1,0:T(8,128)S(1)}, f32[40,128]{1,0:T(8,128)S(1)}, u32[]{:S(2)}, u32[]{:S(2)}) collective-permute-start(f32[40,128]{1,0:T(8,128)S(1)} %get-tuple-element.26), channel_id=1, source_target_pairs={{0,3},{1,2},{2,1},{3,0},{4,7},{5,6},{6,5},{7,4},{8,11},{9,10},{10,... | collective-permute-start | bytes 61448 | tf_op jit(solution)/shard_map/ppermute | solution.py:408
  5.2 0.0 collective-permute-start.2
  5.3 2.0 %collective-permute-start.3 = (f32[11,8,128]{2,1,0:T(8,128)S(1)}, f32[11,8,128]{2,1,0:T(8,128)S(1)}, u32[]{:S(2)}, u32[]{:S(2)}) collective-permute-start(f32[11,8,128]{2,1,0:T(8,128)S(1)} %get-tuple-element.29), channel_id=1, source_target_pairs={{0,4},{4,8},{8,12},{12,16},{16,20},{20,24},{24,28},{28,0},{1,5},{5... | collective-permute-start | bytes 135176 | tf_op jit(solution)/shard_map/ppermute | solution.py:416
  7.3 1.6 %collective-permute-done.2.refs_5_ = f32[8,128]{1,0:T(8,128)S(1)} collective-permute-done((f32[8,128]{1,0:T(8,128)S(1)}, f32[8,128]{1,0:T(8,128)S(1)}, u32[]{:S(2)}, u32[]{:S(2)}) %collective-permute-start.2) | collective-permute-done | bytes 4128 | tf_op jit(solution)/shard_map/ppermute | solution.py:412
  8.8 0.0 collective-permute-done.refs_1_
  8.8 0.0 collective-permute-done.1.refs_2_
  8.8 0.2 second.1
  9.0 4.6 %collective-permute-start.5 = (f32[11,8,128]{2,1,0:T(8,128)S(1)}, f32[11,8,128]{2,1,0:T(8,128)S(1)}, u32[]{:S(2)}, u32[]{:S(2)}) collective-permute-start(f32[11,8,128]{2,1,0:T(8,128)S(1)} %get-tuple-element.31), channel_id=1, source_target_pairs={{0,28},{4,0},{8,4},{12,8},{16,12},{20,16},{24,20},{28,24},{1,29},{... | collective-permute-start | bytes 135176 | tf_op jit(solution)/shard_map/ppermute | solution.py:431
  13.7 0.0 collective-permute-start.4
  13.7 0.8 %inner.1.held_h = f32[27,2,8,128]{3,2,1,0:T(8,128)} custom-call(f32[27,2,8,128]{3,2,1,0:T(8,128)S(1)} %get-tuple-element.28.post, f32[40,128]{1,0:T(8,128)S(1)} %get-tuple-element.32.edge, f32[3,2,8,128]{3,2,1,0:T(8,128)S(1)} %get-tuple-element.27.refs_4_.maps), custom_call_target="tpu_custom_call" | custom-call | tf_op jit(solution)/shard_map/inner/pallas_call | solution.py:432
  14.4 5.6 %collective-permute-done.4.below = f32[4,8,128]{2,1,0:T(8,128)S(1)} collective-permute-done((f32[4,8,128]{2,1,0:T(8,128)S(1)}, f32[4,8,128]{2,1,0:T(8,128)S(1)}, u32[]{:S(2)}, u32[]{:S(2)}) %collective-permute-start.4) | collective-permute-done | bytes 16416 | tf_op jit(solution)/shard_map/ppermute | solution.py:430
  20.1 0.0 collective-permute-done.3.early
  20.1 0.0 collective-permute-done.5.above
  20.1 0.7 %outer.1 = f32[27,2,8,128]{3,2,1,0:T(8,128)} custom-call(f32[27,2,8,128]{3,2,1,0:T(8,128)S(1)} %get-tuple-element.28.post, f32[11,8,128]{2,1,0:T(8,128)S(1)} %collective-permute-done.3.early, f32[4,8,128]{2,1,0:T(8,128)S(1)} %collective-permute-done.4.below, f32[11,8,128]{2,1,0:T(8,128)S(1)} %collective-permute-done.5.above, ...), custom_call_target="tpu_custom_call", output_to_operand_aliasing={{}: (4, {})} | custom-call | tf_op jit(solution)/shard_map/outer/pallas_call | solution.py:441
  (3 shorter events, 0.0 us)
Async XLA Ops:
  0.0 1.0 %copy-start = (f32[27,2,8,128]{3,2,1,0:T(8,128)S(1)}, f32[27,2,8,128]{3,2,1,0:T(8,128)}, u32[]{:S(2)}) copy-start(f32[27,2,8,128]{3,2,1,0:T(8,128)} %pop.1) | copy-start | bytes 663556
  0.0 0.8 %copy-start.4 = (s32[1,1,256]{2,1,0:T(1,128)S(1)}, s32[1,1,256]{2,1,0:T(1,128)}, u32[]{:S(2)}) copy-start(s32[1,1,256]{2,1,0:T(1,128)} %cell.1) | copy-start | bytes 3076
  0.0 0.8 %copy-start.5 = (s32[1,1,256]{2,1,0:T(1,128)S(1)}, s32[1,1,256]{2,1,0:T(1,128)}, u32[]{:S(2)}) copy-start(s32[1,1,256]{2,1,0:T(1,128)} %normal.1) | copy-start | bytes 3076
  0.0 0.8 %copy-start.6 = (s32[1,1,256]{2,1,0:T(1,128)S(1)}, s32[1,1,256]{2,1,0:T(1,128)}, u32[]{:S(2)}) copy-start(s32[1,1,256]{2,1,0:T(1,128)} %ref.1) | copy-start | bytes 3076
  0.0 0.8 %copy-start.7 = (f32[27]{0:T(128)S(1)}, f32[27]{0:T(128)}, u32[]{:S(2)}) copy-start(f32[27]{0:T(128)} %param.10) | copy-start | bytes 328
  0.0 1.0 %copy-start.3 = (f32[1,1,8,256]{3,2,1,0:T(8,128)S(1)}, f32[1,1,8,256]{3,2,1,0:T(8,128)}, u32[]{:S(2)}) copy-start(f32[1,1,8,256]{3,2,1,0:T(8,128)} %sweight.1) | copy-start | bytes 24580
  0.0 1.0 %copy-start.2 = (s32[1,1,8,256]{3,2,1,0:T(8,128)S(1)}, s32[1,1,8,256]{3,2,1,0:T(8,128)}, u32[]{:S(2)}) copy-start(s32[1,1,8,256]{3,2,1,0:T(8,128)} %scell.1) | copy-start | bytes 24580
  1.2 0.7 %copy-start.1 = (s32[2,8,128]{2,1,0:T(8,128)S(1)}, s32[2,8,128]{2,1,0:T(8,128)}, u32[]{:S(2)}) copy-start(s32[2,8,128]{2,1,0:T(8,128)} %refs_3_.1) | copy-start | bytes 24580
  2.1 6.7 %collective-permute-start = (f32[40,128]{1,0:T(8,128)S(1)}, f32[40,128]{1,0:T(8,128)S(1)}, u32[]{:S(2)}, u32[]{:S(2)}) collective-permute-start(f32[40,128]{1,0:T(8,128)S(1)} %get-tuple-element.25), channel_id=1, source_target_pairs={{0,1},{1,0},{2,3},{3,2},{4,5},{5,4},{6,7},{7,6},{8,9},{9,8},{10,11... | collective-permute-start | bytes 61448 | tf_op jit(solution)/shard_map/ppermute | solution.py:408
  2.6 6.2 %collective-permute-start.1 = (f32[40,128]{1,0:T(8,128)S(1)}, f32[40,128]{1,0:T(8,128)S(1)}, u32[]{:S(2)}, u32[]{:S(2)}) collective-permute-start(f32[40,128]{1,0:T(8,128)S(1)} %get-tuple-element.26), channel_id=1, source_target_pairs={{0,3},{1,2},{2,1},{3,0},{4,7},{5,6},{6,5},{7,4},{8,11},{9,10},{10,... | collective-permute-start | bytes 61448 | tf_op jit(solution)/shard_map/ppermute | solution.py:408
  5.2 3.6 %collective-permute-start.2 = (f32[8,128]{1,0:T(8,128)S(1)}, f32[8,128]{1,0:T(8,128)S(1)}, u32[]{:S(2)}, u32[]{:S(2)}) collective-permute-start(f32[8,128]{1,0:T(8,128)S(1)} %get-tuple-element.20.refs_5_.refs_0_), channel_id=1, source_target_pairs={{0,2},{1,3},{2,0},{3,1},{4,6},{5,7},{6,4},{7,5},{8,10},{9,11},{10,... | collective-permute-start | bytes 12296 | tf_op jit(solution)/shard_map/ppermute | solution.py:412
  5.3 14.8 %collective-permute-start.3 = (f32[11,8,128]{2,1,0:T(8,128)S(1)}, f32[11,8,128]{2,1,0:T(8,128)S(1)}, u32[]{:S(2)}, u32[]{:S(2)}) collective-permute-start(f32[11,8,128]{2,1,0:T(8,128)S(1)} %get-tuple-element.29), channel_id=1, source_target_pairs={{0,4},{4,8},{8,12},{12,16},{16,20},{20,24},{24,28},{28,0},{1,5},{5... | collective-permute-start | bytes 135176 | tf_op jit(solution)/shard_map/ppermute | solution.py:416
  9.0 11.1 %collective-permute-start.5 = (f32[11,8,128]{2,1,0:T(8,128)S(1)}, f32[11,8,128]{2,1,0:T(8,128)S(1)}, u32[]{:S(2)}, u32[]{:S(2)}) collective-permute-start(f32[11,8,128]{2,1,0:T(8,128)S(1)} %get-tuple-element.31), channel_id=1, source_target_pairs={{0,28},{4,0},{8,4},{12,8},{16,12},{20,16},{24,20},{28,24},{1,29},{... | collective-permute-start | bytes 135176 | tf_op jit(solution)/shard_map/ppermute | solution.py:431
  13.7 6.4 %collective-permute-start.4 = (f32[4,8,128]{2,1,0:T(8,128)S(1)}, f32[4,8,128]{2,1,0:T(8,128)S(1)}, u32[]{:S(2)}, u32[]{:S(2)}) collective-permute-start(f32[4,8,128]{2,1,0:T(8,128)S(1)} %get-tuple-element.30), channel_id=1, source_target_pairs={{0,4},{4,8},{8,12},{12,16},{16,20},{20,24},{24,28},{28,0},{1,5},{5... | collective-permute-start | bytes 49160 | tf_op jit(solution)/shard_map/ppermute | solution.py:430

commit v5 on v4

--- a/solution.py
+++ b/solution.py
@@ -14,6 +14,7 @@
 FACE = 16
 HBM = pl.BlockSpec(memory_space=pltpu.HBM)
 VMEM = pl.BlockSpec(memory_space=pltpu.VMEM)
+THROUGH = ("normal", "ref", "relax")
 COVER = 4 * 10**9
 GRANT = 4 * 1024 * 1024
 
@@ -115,16 +116,16 @@
     out[...] = lax.broadcasted_iota(jnp.int32, out.shape, 1)
 
 
-def live_kernel(number, cell, normal, ref, relax, count, cell_o, axis_o, ref_o, keep_o):
-    cell_o[...] = jnp.where(number[...] < count[0, 0], cell[0], -1)
-    axis_o[...] = normal[0] // 2
-    ref_o[...] = ref[0]
-    keep_o[...] = 1.0 - relax[...]
-
-
-def cell_kernel(keep, pop, scell, sweight, state_o, sample_o):
+def live_kernel(number, count, cell, *rest):
+    half = (len(rest) - 1) // 2
+    rest[half][...] = jnp.where(number[...] < count[0, 0], cell[0], -1)
+    for source, target in zip(rest[:half], rest[half + 1 :]):
+        target[...] = source[...]
+
+
+def cell_kernel(relax, pop, scell, sweight, state_o, sample_o):
     size_x, slots = pop.shape[1], scell.shape[-1]
-    rates = [jnp.broadcast_to(keep[0:1, i : i + 1], (ROWS, LANES)) for i in range(27)]
+    rates = [1.0 - jnp.broadcast_to(relax[0:1, i : i + 1], (ROWS, LANES)) for i in range(27)]
     velocity = []
     for x in range(size_x):
         density, vel, kept = relaxed([pop[i, x] for i in range(27)], rates)
@@ -161,12 +162,12 @@
             sample_o[r : r + 1, :] = jnp.sum(total[d], axis=0, keepdims=True)
 
 
-def face_kernel(cell, axis, ref, solid, state, sample, even_o, odd_o, early_o, map_o, *, gy):
+def face_kernel(cell, normal, ref, solid, state, sample, even_o, odd_o, early_o, map_o, *, gy):
     size_x, walls = solid.shape[0], cell.shape[-1]
     row = jnp.where(cell[...] < 0, -1, cell[...] // LANES)
     z = cell[...] % LANES
-    low = (ref[...] % LANES + 1).astype(jnp.float32)
-    high = (ref[...] // LANES * 4 + axis[...]).astype(jnp.float32)
+    low = (ref[0] % LANES + 1).astype(jnp.float32)
+    high = (ref[0] // LANES * 4 + normal[0] // 2).astype(jnp.float32)
     height = size_x * ROWS
     at = lax.broadcasted_iota(jnp.int32, (height, walls), 0) == jnp.broadcast_to(row, (height, walls))
     left = jnp.concatenate(
@@ -199,6 +200,13 @@
         odd_o[base + n : base + n + 1, :] = jnp.where(parity == 0, below, above)
 
 
+def first_kernel(
+    cells, normal, ref, relax, solid, scell, sweight, pop, even_o, odd_o, sample_o, state_o, early_o, map_o, *, gy
+):
+    cell_kernel(relax, pop, scell, sweight, state_o, sample_o)
+    face_kernel(cells, normal, ref, solid, state_o, sample_o, even_o, odd_o, early_o, map_o, gy=gy)
+
+
 def second_kernel(own, y_even, y_odd, *rest, gy, peers, slots, slots_each):
     state, maps, rest = rest[0], rest[1], rest[2:]
     far, outs = rest[: peers - 3], rest[peers - 3 :]
@@ -373,36 +381,35 @@
         compiler_params=pltpu.CompilerParams(vmem_limit_bytes=GRANT),
         name="number",
     )()
-    wall_row = jax.ShapeDtypeStruct((1, walls), jnp.int32)
-    cells, axis, refs, keep = pl.pallas_call(
+    taken = {
+        "normal": wall_normal, "ref": sample_ref, "relax": relax.reshape(1, 27),
+        "solid": solid, "scell": stencil_cell, "sweight": stencil_weight,
+    }
+    passed = [taken[name] for name in THROUGH]
+    cells, *passed = pl.pallas_call(
         live_kernel,
-        out_shape=[wall_row, wall_row, wall_row, jax.ShapeDtypeStruct((1, 27), f32)],
-        in_specs=[VMEM] * 5 + [pl.BlockSpec(memory_space=pltpu.SMEM)],
-        out_specs=[VMEM] * 4,
+        out_shape=[jax.ShapeDtypeStruct(v.shape, v.dtype) for v in (number, *passed)],
+        in_specs=[VMEM, pl.BlockSpec(memory_space=pltpu.SMEM)] + [VMEM] * (1 + len(passed)),
+        out_specs=[VMEM] * (1 + len(passed)),
         compiler_params=pltpu.CompilerParams(vmem_limit_bytes=GRANT),
         name="live",
-    )(number, wall_cell, wall_normal, sample_ref, relax.reshape(1, 27), wall_count)
-    state, samples = pl.pallas_call(
-        cell_kernel,
-        out_shape=[jax.ShapeDtypeStruct((PLANES, *block), f32), jax.ShapeDtypeStruct((lines, LANES), f32)],
-        in_specs=[VMEM] * 4,
-        out_specs=[VMEM] * 2,
-        compiler_params=pltpu.CompilerParams(vmem_limit_bytes=GRANT),
-        name="cells",
-    )(keep, populations, stencil_cell, stencil_weight)
-    y_even, y_odd, early, maps = pl.pallas_call(
-        lambda *refs: face_kernel(*refs, gy="gy"),
+    )(number, wall_count, wall_cell, *passed)
+    taken.update(zip(THROUGH, passed))
+    y_even, y_odd, samples, state, early, maps = pl.pallas_call(
+        lambda *refs: first_kernel(*refs, gy="gy"),
         out_shape=[
             jax.ShapeDtypeStruct(face, f32),
             jax.ShapeDtypeStruct(face, f32),
+            jax.ShapeDtypeStruct((lines, LANES), f32),
+            jax.ShapeDtypeStruct((PLANES, *block), f32),
             jax.ShapeDtypeStruct((11, ROWS, LANES), f32),
             jax.ShapeDtypeStruct((3, *block), f32),
         ],
-        in_specs=[VMEM] * 6,
-        out_specs=[VMEM] * 4,
-        compiler_params=pltpu.CompilerParams(vmem_limit_bytes=GRANT),
-        name="face",
-    )(cells, axis, refs, solid, state, samples)
+        in_specs=[VMEM] * 8,
+        out_specs=[VMEM] * 6,
+        compiler_params=pltpu.CompilerParams(vmem_limit_bytes=GRANT),
+        name="first",
+    )(cells, *taken.values(), populations)
 
     def swap(value, odd):
         return lax.ppermute(value, "gy", [(i, (((i - odd) ^ 1) + odd) % peers) for i in range(peers)])

time: 21 us -> 20.1 us (0.957)
  local copies, waits for them, and re-layouts: 0.85 us -> 0.12 us
    unnamed x16, local copies, waits for them, and re-layouts: 0.85 us -> 0.12 us
where the time goes in v5:
time: 20.1 us; the launch traced here: 20 us
  starting transfers between devices  9.81 us (49%)
  waiting for transfers between devices  7.21 us (36%)
  Pallas kernels  1.95 us (10%)
  between operations  0.9 us (4%)
    ppermute x1, waiting for transfers between devices, local(): from_below = lax.ppermute(plus, 'gx', ring)  5.65 us
    ppermute x1, starting transfers between devices, local(): lax.ppermute(minus, 'gx', [(i, (i - 1) % devices) for i in range(devices)])  4.61 us
    ppermute x2, starting transfers between devices, swap(): lax.ppermute(value, 'gy', [(i, ((i - odd ^ 1) + odd) % peers) for i in ra...  3.14 us
    ppermute x1, starting transfers between devices, local(): early = lax.ppermute(early, 'gx', ring)  2.01 us
    ppermute x1, waiting for transfers between devices, local(): lax.ppermute(samples, 'gy', [(i, (i + n) % peers) for i in range(peers)])  1.55 us
    pallas_call x1, Pallas kernels, local(): pl.pallas_call(inner_kernel, out_shape=jax.ShapeDtypeStruct(populations.s...  0.78 us
    pallas_call x1, Pallas kernels, local(): pl.pallas_call(outer_kernel, out_shape=jax.ShapeDtypeStruct(populations.s...  0.73 us
  transfers between devices with their start and end apart: 6, of which 2 were waited for; matrix products, arithmetic and copies ran while one was open for 0% of the time, Pallas kernels for 5%

profile of v5, /device:TPU:0, one launch (start us, length us, event | category | flops | bytes accessed | tf_op | source)
XLA Modules:
  0.0 20.0 jit_solution(16732568166757793715)
XLA Ops:
  0.0 0.0 copy-start.4
  0.0 0.0 copy-start.5
  0.0 0.0 copy-start.6
  0.0 0.0 copy-start.7
  0.0 0.0 copy-start
  0.0 0.0 copy-start.3
  0.0 0.0 copy-start.1
  0.1 0.0 copy-start.2
  0.9 0.0 copy-done.4
  0.9 0.0 copy-done.5
  0.9 0.0 copy-done.6
  0.9 0.0 copy-done.7
  0.9 0.1 copy-done
  1.0 0.0 copy-done.3
  1.0 0.0 copy-done.1
  1.0 0.0 copy-done.2
  1.0 0.2 %first.1 = (f32[40,128]{1,0:T(8,128)S(1)}, f32[40,128]{1,0:T(8,128)S(1)}, f32[8,128]{1,0:T(8,128)S(1)}, f32[31,2,8,128]{3,2,1,0:T(8,128)S(1)}, f32[11,8,128]{2,1,0:T(8,128)S(1)}, /*index=5*/f32[3,2,8,128]{3,2,1,0:T(8,128)S(1)}) custom-call(s32[1,256]{1,0:T(1,128)S(1)} %get-tuple-element.19.refs_0_, s32[1,1,256]{2,1,0:T(1,128)S(1)} %get-tuple-element.20.refs_1_, ...), custom_call_target="tpu_custom_call" | custom-call | tf_op jit(solution)/shard_map/first/pallas_call | solution.py:398
  1.2 0.6 %collective-permute-start = (f32[40,128]{1,0:T(8,128)S(1)}, f32[40,128]{1,0:T(8,128)S(1)}, u32[]{:S(2)}, u32[]{:S(2)}) collective-permute-start(f32[40,128]{1,0:T(8,128)S(1)} %get-tuple-element.24), channel_id=1, source_target_pairs={{0,1},{1,0},{2,3},{3,2},{4,5},{5,4},{6,7},{7,6},{8,9},{9,8},{10,11... | collective-permute-start | bytes 61448 | tf_op jit(solution)/shard_map/ppermute | solution.py:415
  1.8 2.6 %collective-permute-start.1 = (f32[40,128]{1,0:T(8,128)S(1)}, f32[40,128]{1,0:T(8,128)S(1)}, u32[]{:S(2)}, u32[]{:S(2)}) collective-permute-start(f32[40,128]{1,0:T(8,128)S(1)} %get-tuple-element.25), channel_id=1, source_target_pairs={{0,3},{1,2},{2,1},{3,0},{4,7},{5,6},{6,5},{7,4},{8,11},{9,10},{10,... | collective-permute-start | bytes 61448 | tf_op jit(solution)/shard_map/ppermute | solution.py:415
  4.4 0.0 collective-permute-start.2
  4.4 2.0 %collective-permute-start.3 = (f32[11,8,128]{2,1,0:T(8,128)S(1)}, f32[11,8,128]{2,1,0:T(8,128)S(1)}, u32[]{:S(2)}, u32[]{:S(2)}) collective-permute-start(f32[11,8,128]{2,1,0:T(8,128)S(1)} %get-tuple-element.29), channel_id=1, source_target_pairs={{0,4},{4,8},{8,12},{12,16},{16,20},{20,24},{24,28},{28,0},{1,5},{5... | collective-permute-start | bytes 135176 | tf_op jit(solution)/shard_map/ppermute | solution.py:423
  6.4 1.6 %collective-permute-done.2.refs_5_ = f32[8,128]{1,0:T(8,128)S(1)} collective-permute-done((f32[8,128]{1,0:T(8,128)S(1)}, f32[8,128]{1,0:T(8,128)S(1)}, u32[]{:S(2)}, u32[]{:S(2)}) %collective-permute-start.2) | collective-permute-done | bytes 4128 | tf_op jit(solution)/shard_map/ppermute | solution.py:419
  8.0 0.0 collective-permute-done.refs_1_
  8.0 0.0 collective-permute-done.1.refs_2_
  8.0 0.2 second.1
  8.2 4.6 %collective-permute-start.5 = (f32[11,8,128]{2,1,0:T(8,128)S(1)}, f32[11,8,128]{2,1,0:T(8,128)S(1)}, u32[]{:S(2)}, u32[]{:S(2)}) collective-permute-start(f32[11,8,128]{2,1,0:T(8,128)S(1)} %get-tuple-element.31), channel_id=1, source_target_pairs={{0,28},{4,0},{8,4},{12,8},{16,12},{20,16},{24,20},{28,24},{1,29},{... | collective-permute-start | bytes 135176 | tf_op jit(solution)/shard_map/ppermute | solution.py:438
  12.8 0.0 collective-permute-start.4
  12.8 0.8 %inner.1.held_h = f32[27,2,8,128]{3,2,1,0:T(8,128)} custom-call(f32[27,2,8,128]{3,2,1,0:T(8,128)S(1)} %get-tuple-element.28.post, f32[40,128]{1,0:T(8,128)S(1)} %get-tuple-element.32.edge, f32[3,2,8,128]{3,2,1,0:T(8,128)S(1)} %get-tuple-element.27.refs_4_.maps), custom_call_target="tpu_custom_call" | custom-call | tf_op jit(solution)/shard_map/inner/pallas_call | solution.py:439
  13.6 5.6 %collective-permute-done.4.below = f32[4,8,128]{2,1,0:T(8,128)S(1)} collective-permute-done((f32[4,8,128]{2,1,0:T(8,128)S(1)}, f32[4,8,128]{2,1,0:T(8,128)S(1)}, u32[]{:S(2)}, u32[]{:S(2)}) %collective-permute-start.4) | collective-permute-done | bytes 16416 | tf_op jit(solution)/shard_map/ppermute | solution.py:437
  19.2 0.0 collective-permute-done.3.early
  19.2 0.0 collective-permute-done.5.above
  19.3 0.7 %outer.1 = f32[27,2,8,128]{3,2,1,0:T(8,128)} custom-call(f32[27,2,8,128]{3,2,1,0:T(8,128)S(1)} %get-tuple-element.28.post, f32[11,8,128]{2,1,0:T(8,128)S(1)} %collective-permute-done.3.early, f32[4,8,128]{2,1,0:T(8,128)S(1)} %collective-permute-done.4.below, f32[11,8,128]{2,1,0:T(8,128)S(1)} %collective-permute-done.5.above, ...), custom_call_target="tpu_custom_call", output_to_operand_aliasing={{}: (4, {})} | custom-call | tf_op jit(solution)/shard_map/outer/pallas_call | solution.py:448
  (2 shorter events, 0.0 us)
Async XLA Ops:
  0.0 0.9 %copy-start.4 = (s32[1,1,256]{2,1,0:T(1,128)S(1)}, s32[1,1,256]{2,1,0:T(1,128)}, u32[]{:S(2)}) copy-start(s32[1,1,256]{2,1,0:T(1,128)} %cell.1) | copy-start | bytes 3076
  0.0 0.9 %copy-start.5 = (s32[1,1,256]{2,1,0:T(1,128)S(1)}, s32[1,1,256]{2,1,0:T(1,128)}, u32[]{:S(2)}) copy-start(s32[1,1,256]{2,1,0:T(1,128)} %rest_0_.1) | copy-start | bytes 3076
  0.0 0.9 %copy-start.6 = (s32[1,1,256]{2,1,0:T(1,128)S(1)}, s32[1,1,256]{2,1,0:T(1,128)}, u32[]{:S(2)}) copy-start(s32[1,1,256]{2,1,0:T(1,128)} %rest_1_.1) | copy-start | bytes 3076
  0.0 0.9 %copy-start.7 = (f32[27]{0:T(128)S(1)}, f32[27]{0:T(128)}, u32[]{:S(2)}) copy-start(f32[27]{0:T(128)} %param.10) | copy-start | bytes 328
  0.0 1.0 %copy-start = (f32[27,2,8,128]{3,2,1,0:T(8,128)S(1)}, f32[27,2,8,128]{3,2,1,0:T(8,128)}, u32[]{:S(2)}) copy-start(f32[27,2,8,128]{3,2,1,0:T(8,128)} %refs_7_.1) | copy-start | bytes 663556
  0.0 1.0 %copy-start.3 = (f32[1,1,8,256]{3,2,1,0:T(8,128)S(1)}, f32[1,1,8,256]{3,2,1,0:T(8,128)}, u32[]{:S(2)}) copy-start(f32[1,1,8,256]{3,2,1,0:T(8,128)} %refs_6_.1) | copy-start | bytes 24580
  0.0 1.0 %copy-start.1 = (s32[2,8,128]{2,1,0:T(8,128)S(1)}, s32[2,8,128]{2,1,0:T(8,128)}, u32[]{:S(2)}) copy-start(s32[2,8,128]{2,1,0:T(8,128)} %refs_4_.1) | copy-start | bytes 24580
  0.1 1.0 %copy-start.2 = (s32[1,1,8,256]{3,2,1,0:T(8,128)S(1)}, s32[1,1,8,256]{3,2,1,0:T(8,128)}, u32[]{:S(2)}) copy-start(s32[1,1,8,256]{3,2,1,0:T(8,128)} %refs_5_.1) | copy-start | bytes 24580
  1.2 6.8 %collective-permute-start = (f32[40,128]{1,0:T(8,128)S(1)}, f32[40,128]{1,0:T(8,128)S(1)}, u32[]{:S(2)}, u32[]{:S(2)}) collective-permute-start(f32[40,128]{1,0:T(8,128)S(1)} %get-tuple-element.24), channel_id=1, source_target_pairs={{0,1},{1,0},{2,3},{3,2},{4,5},{5,4},{6,7},{7,6},{8,9},{9,8},{10,11... | collective-permute-start | bytes 61448 | tf_op jit(solution)/shard_map/ppermute | solution.py:415
  1.8 6.2 %collective-permute-start.1 = (f32[40,128]{1,0:T(8,128)S(1)}, f32[40,128]{1,0:T(8,128)S(1)}, u32[]{:S(2)}, u32[]{:S(2)}) collective-permute-start(f32[40,128]{1,0:T(8,128)S(1)} %get-tuple-element.25), channel_id=1, source_target_pairs={{0,3},{1,2},{2,1},{3,0},{4,7},{5,6},{6,5},{7,4},{8,11},{9,10},{10,... | collective-permute-start | bytes 61448 | tf_op jit(solution)/shard_map/ppermute | solution.py:415
  4.4 3.6 %collective-permute-start.2 = (f32[8,128]{1,0:T(8,128)S(1)}, f32[8,128]{1,0:T(8,128)S(1)}, u32[]{:S(2)}, u32[]{:S(2)}) collective-permute-start(f32[8,128]{1,0:T(8,128)S(1)} %get-tuple-element.23.refs_0_), channel_id=1, source_target_pairs={{0,2},{1,3},{2,0},{3,1},{4,6},{5,7},{6,4},{7,5},{8,10},{9,11},{10,... | collective-permute-start | bytes 12296 | tf_op jit(solution)/shard_map/ppermute | solution.py:419
  4.4 14.8 %collective-permute-start.3 = (f32[11,8,128]{2,1,0:T(8,128)S(1)}, f32[11,8,128]{2,1,0:T(8,128)S(1)}, u32[]{:S(2)}, u32[]{:S(2)}) collective-permute-start(f32[11,8,128]{2,1,0:T(8,128)S(1)} %get-tuple-element.29), channel_id=1, source_target_pairs={{0,4},{4,8},{8,12},{12,16},{16,20},{20,24},{24,28},{28,0},{1,5},{5... | collective-permute-start | bytes 135176 | tf_op jit(solution)/shard_map/ppermute | solution.py:423
  8.2 11.1 %collective-permute-start.5 = (f32[11,8,128]{2,1,0:T(8,128)S(1)}, f32[11,8,128]{2,1,0:T(8,128)S(1)}, u32[]{:S(2)}, u32[]{:S(2)}) collective-permute-start(f32[11,8,128]{2,1,0:T(8,128)S(1)} %get-tuple-element.31), channel_id=1, source_target_pairs={{0,28},{4,0},{8,4},{12,8},{16,12},{20,16},{24,20},{28,24},{1,29},{... | collective-permute-start | bytes 135176 | tf_op jit(solution)/shard_map/ppermute | solution.py:438
  12.8 6.4 %collective-permute-start.4 = (f32[4,8,128]{2,1,0:T(8,128)S(1)}, f32[4,8,128]{2,1,0:T(8,128)S(1)}, u32[]{:S(2)}, u32[]{:S(2)}) collective-permute-start(f32[4,8,128]{2,1,0:T(8,128)S(1)} %get-tuple-element.30), channel_id=1, source_target_pairs={{0,4},{4,8},{8,12},{12,16},{16,20},{20,24},{24,28},{28,0},{1,5},{5... | collective-permute-start | bytes 49160 | tf_op jit(solution)/shard_map/ppermute | solution.py:437
